TPU v7x, 32 devices: a whole 2x2x4 slice. The times are simulated.
32 devices in a mesh: dom: 32 (over z, y, x, core).
Axes of the slice: x: 2, y: 2, z: 4, core: 2. Of those that a mesh axis runs over, the one named last changes fastest.
Arguments:
- features: bfloat16 [8192, 512], P('dom'), may hold values from -6 to 6
- w_one: bfloat16 [9, 512, 512], replicated, may hold values from -0.25 to 0.25
- w_two: bfloat16 [8, 512, 349], replicated, may hold values from -0.25 to 0.25
- self_two: bfloat16 [512, 349], replicated, may hold values from -80 to 80
- edge_src: int32 [8, 64, 256], P(None, 'dom'), may hold values from 0 to 511, as said below
- edge_dst: int32 [8, 64, 256], P(None, 'dom'), may hold values from -1 to 127, as said below
- send_rows: int32 [32, 32, 8], P('dom'), may hold values from 0 to 255
- send_count: int32 [32, 32], P('dom'), may hold values from 1 to 8, as said below
- labels: int32 [8192], P('dom'), may hold values from -1 to 348
Outputs:
- logits: float32 [8192, 349], P('dom')
- loss: float32 [], replicated
- grad_one: float32 [4608, 512], P('dom')
- grad_two: float32 [4608, 349], P('dom')
Inputs may be any that keep to these rules, and one draw needn't show every extreme that they name: `send_rows`: entry [p, q, s] is a row of partition p's own nodes, rows may repeat. `send_count`: entry [p, q] counts the live slots p sends to q; every row reaches 8 at some q. `edge_src`: index into the destination partition's table: its 256 own rows, then 8 slots from each partition in order. `edge_dst`: -1 marks an empty edge slot.
All inputs are finite; a program needn't handle non-finite values.
Results may differ from a plain program's by a relative error of at most 0.0085.
The roundings to bfloat16 on the way count: a program that leaves them out, or rounds other values in their place, can miss the bound.
Values may be sent and summed in bfloat16 or wider, within the bound.
No kernel may reach another device: no remote copies, remote signals or barrier semaphores. Data moves between devices by JAX's collectives and lax.ppermute only.
A program may use at most 128 MiB of HBM per device.

v0:
```python
import functools

import jax
import jax.numpy as jnp
from jax import lax
from jax.experimental import pallas as pl
from jax.experimental.pallas import tpu as pltpu
from jax.sharding import PartitionSpec as P


loss_scale = 256.0
bf16 = jnp.bfloat16
f32 = jnp.float32
EXTRA = 128


def dot(a, b):
    return jnp.dot(a, b, preferred_element_type=f32)


def dot_nt(a, b):
    return lax.dot_general(a, b, (((1,), (1,)), ((), ())), preferred_element_type=f32)


def dot_tn(a, b):
    return lax.dot_general(a, b, (((0,), (0,)), ((), ())), preferred_element_type=f32)


def iota(shape, axis):
    return lax.broadcasted_iota(jnp.int32, shape, axis)


HBM = pltpu.HBM
ALL_VMEM = 67043328


def call(body, outs, ins, spaces, out_spaces, scratch=(), copies=0, flops=0, moved=0, vmem=0):
    kinds = {"v": pltpu.VMEM, "h": pl.ANY, "s": pltpu.SMEM}
    out_kinds = {"v": pltpu.VMEM, "h": HBM}
    scratch = list(scratch)
    if copies:
        scratch.append(pltpu.SemaphoreType.DMA((copies,)))
    return pl.pallas_call(
        body,
        out_shape=[jax.ShapeDtypeStruct(s, d) for s, d in outs],
        in_specs=[pl.BlockSpec(memory_space=kinds[c]) for c in spaces],
        out_specs=[pl.BlockSpec(memory_space=out_kinds[c]) for c in out_spaces],
        scratch_shapes=scratch,
        compiler_params=pltpu.CompilerParams(vmem_limit_bytes=vmem << 20 or ALL_VMEM),
        cost_estimate=pl.CostEstimate(flops=flops, bytes_accessed=moved, transcendentals=0),
    )(*ins)


class Copies:
    def __init__(self, sems):
        self.sems, self.used = sems, 0

    def start(self, source, target):
        copy = pltpu.make_async_copy(source, target, self.sems.at[self.used])
        self.used += 1
        copy.start()
        return copy


def wait_all(copies):
    for copy in copies:
        copy.wait()


def pick_hot(picks, counts, rows):
    slots, peers = picks.shape
    chosen = jnp.where(iota((slots, peers), 0) < counts, picks, -1).astype(f32)
    lane = iota((peers, peers * slots), 1)
    spreader = jnp.where(iota((peers, peers * slots), 0) == lane // slots, 1.0, 0.0)
    laid = jnp.dot(chosen, spreader, preferred_element_type=f32, precision=lax.Precision.HIGHEST)
    mine = iota((slots, peers * slots), 0) == iota((slots, peers * slots), 1) % slots
    row = jnp.sum(jnp.where(mine, laid, 0.0), axis=0, keepdims=True)
    hot = iota((rows, peers * slots), 0) == jnp.round(row).astype(jnp.int32)
    return jnp.where(hot, 1.0, 0.0).astype(bf16)


def pack_kernel(feat_hbm, picks_hbm, count_hbm, label_hbm, out_ref, feat, picks, counts, label, sems):
    copies = Copies(sems)
    pairs = ((picks_hbm, picks), (count_hbm, counts), (label_hbm, label), (feat_hbm, feat))
    wait_all([copies.start(a, b) for a, b in pairs])
    rows, width = feat.shape
    slots = out_ref.shape[0]
    hot = pick_hot(picks[...], counts[...], rows)
    out_ref[:, :width] = dot_tn(hot, feat[...]).astype(bf16)
    count = jnp.sum(jnp.where(label[...] >= 0, 1.0, 0.0), axis=1, keepdims=True)
    high = jnp.floor(count * (1.0 / 128.0))
    low = count - 128.0 * high
    lane = iota((slots, EXTRA), 1)
    out_ref[:, width:] = jnp.where(lane < 64, high, low).astype(bf16)


def graph_kernel(
    src_hbm, dst_hbm, adj_hbm, norm_hbm, back_hbm, src_ref, dst_ref, adj_ref, norm_ref, back_ref, sems
):
    copies = Copies(sems)
    wait_all([copies.start(src_hbm, src_ref), copies.start(dst_hbm, dst_ref)])
    relations, blocks, edges = src_ref.shape
    table = adj_ref.shape[1]

    def step(r, carry):
        for b in range(blocks):
            start = pl.multiple_of((r * blocks + b) * 128, 128)
            src = src_ref[r, b : b + 1, :]
            dst = dst_ref[r, b : b + 1, :]
            hot_dst = jnp.where(iota((128, edges), 0) == dst, 1.0, 0.0)
            hot_src = jnp.where(iota((table, edges), 0) == src, 1.0, 0.0).astype(bf16)
            count = jnp.sum(hot_dst, axis=1, keepdims=True)
            hot_dst = hot_dst.astype(bf16)
            adj_ref[pl.ds(start, 128), :] = dot_nt(hot_dst, hot_src).astype(bf16)
            back_ref[:, pl.ds(start, 128)] = dot_nt(hot_src, hot_dst).astype(bf16)
            norm = 1.0 / jnp.maximum(count, 1.0)
            norm_ref[pl.ds(start, 128), :] = jnp.broadcast_to(norm, (128, EXTRA))
        return carry

    lax.fori_loop(0, relations, step, 0)
    pairs = ((adj_ref, adj_hbm), (norm_ref, norm_hbm), (back_ref, back_hbm))
    wait_all([copies.start(a, b) for a, b in pairs])


def wide(norm, width):
    return jnp.concatenate([norm] * (width // EXTRA), axis=1)


def put_blocks(me, turned, blocks, block):
    pad = blocks.shape[2] - block
    rows = blocks.shape[3]
    for b in range(turned.shape[0] // block):
        place = jnp.bitwise_xor(me, b)
        value = turned[b * block : (b + 1) * block, :].astype(bf16)
        if pad:
            value = jnp.concatenate([value, jnp.zeros((pad, rows), bf16)], axis=0)
        blocks[jnp.bitwise_and(place, 1), jnp.right_shift(place, 1)] = value


def first_kernel(
    adj_hbm, norm_hbm, got_hbm, feat_hbm, w_hbm, picks_hbm, count_hbm,
    left_hbm, hid_hbm, pack_hbm, total_hbm,
    adj, norm, got_ref, feat, w, picks, counts, left, hid, packed, total_ref, sems,
):
    copies = Copies(sems)
    rows, width = feat.shape
    relations = w.shape[0] // width - 1
    chunks = [slice(r * rows, (r + 2) * rows) for r in range(0, relations, 2)]
    near = [copies.start(feat_hbm, feat), copies.start(got_hbm, got_ref)]
    adj_in, norm_in, w_in = [], [], []
    for at in chunks:
        adj_in.append(copies.start(adj_hbm.at[at, :], adj.at[at, :]))
        norm_in.append(copies.start(norm_hbm.at[at, :], norm.at[at, :]))
    parts = [slice(0, 4 * width), slice(4 * width, 7 * width), slice(7 * width, (relations + 1) * width)]
    for at in parts:
        w_in.append(copies.start(w_hbm.at[at, :], w.at[at, :]))
    small = [copies.start(picks_hbm, picks), copies.start(count_hbm, counts)]
    wait_all(near)
    own = feat[...]
    got = got_ref[:, :width]
    left[:, relations * width :] = own
    for i, at in enumerate(chunks):
        adj_in[i].wait()
        norm_in[i].wait()
        sums = dot(adj[at, :rows], own) + dot(adj[at, rows:], got)
        avg = (sums * wide(norm[at, :], width)).astype(bf16)
        left[:, 2 * i * width : (2 * i + 1) * width] = avg[:rows]
        left[:, (2 * i + 1) * width : (2 * i + 2) * width] = avg[rows:]
    out = [copies.start(left, left_hbm)]
    wait_all(small)
    hot = pick_hot(picks[...], counts[...], rows)
    total = None
    for i, at in enumerate(parts):
        w_in[i].wait()
        part = dot(left[:, at], w[at, :])
        total = part if total is None else total + part
    hidden = jnp.maximum(total, 0.0).astype(bf16)
    packed[...] = dot_tn(hot, hidden).astype(bf16)
    out.append(copies.start(packed, pack_hbm))
    hid[...] = hidden
    out.append(copies.start(hid, hid_hbm))
    sums = jnp.sum(got_ref[:, width:].astype(f32), axis=0, keepdims=True)
    count = (sums[:, 0:1] * 128.0 + sums[:, 64:65]) * 0.125
    total_ref[...] = jnp.broadcast_to(count, total_ref.shape)
    out.append(copies.start(total_ref, total_hbm))
    wait_all(out)


def second_kernel(
    block, me_ref, got_hbm, adj_hbm, norm_hbm, back_hbm, hid_hbm, w_hbm, self_hbm, label_hbm, total_hbm,
    logit_hbm, keep_hbm, send_hbm, grad_hbm, local_hbm, out_hbm,
    got_ref, adj, norm, back, hid, w, selfs, label, total, logit, turned, blocks, grad_ref, spreads,
    local_ref, packed, sems,
):
    copies = Copies(sems)
    rows, width = hid.shape
    relations, classes, _ = w.shape
    chunks = [slice(r * rows, (r + 2) * rows) for r in range(0, relations, 2)]
    near = [copies.start(hid_hbm, hid), copies.start(got_hbm, got_ref)]
    adj_in, w_in, norm_in = [], [], []
    for i, at in enumerate(chunks):
        adj_in.append(copies.start(adj_hbm.at[at, :], adj.at[at, :]))
        norm_in.append(copies.start(norm_hbm.at[at, :], norm.at[at, :]))
        w_in.append(copies.start(w_hbm.at[2 * i : 2 * i + 2], w.at[2 * i : 2 * i + 2]))
    small = [copies.start(a, b) for a, b in ((self_hbm, selfs), (label_hbm, label), (total_hbm, total))]
    back_in = copies.start(back_hbm, back)
    wait_all(near)
    own = hid[...]
    got = got_ref[...]
    logits = None
    turned[relations * width :, :] = own.T.astype(turned.dtype)
    for i, at in enumerate(chunks):
        adj_in[i].wait()
        norm_in[i].wait()
        sums = dot(adj[at, :rows], own) + dot(adj[at, rows:], got)
        avg = (sums * wide(norm[at, :], width)).astype(bf16)
        w_in[i].wait()
        part = dot_nt(w[2 * i], avg[:rows]) + dot_nt(w[2 * i + 1], avg[rows:])
        logits = part if logits is None else logits + part
        for j in range(2):
            where = slice((2 * i + j) * width, (2 * i + j + 1) * width)
            turned[where, :] = avg[j * rows : (j + 1) * rows].T.astype(turned.dtype)
    wait_all(small)
    logits = logits + dot_nt(selfs[...], own)
    logit[...] = logits
    out = [copies.start(logit, logit_hbm)]
    put_blocks(me_ref[0], turned, blocks, block)
    out += [copies.start(blocks.at[0], keep_hbm), copies.start(blocks.at[1], send_hbm)]
    count = total[0:1, 0:1]
    labels = label[...]
    labelled = jnp.where(labels >= 0, 1.0, 0.0)
    hot = jnp.where(iota((classes, rows), 0) == labels, 1.0, 0.0)
    peak = jnp.max(logits, axis=0, keepdims=True)
    log_total = peak + jnp.log(jnp.sum(jnp.exp(logits - peak), axis=0, keepdims=True))
    picked = jnp.sum(logits * hot, axis=0, keepdims=True)
    local = jnp.sum(jnp.where(labels >= 0, log_total - picked, 0.0), axis=1, keepdims=True)
    soft = jnp.exp(logits - log_total)
    grad = (loss_scale * (soft - hot) * labelled / count).T.astype(bf16)
    grad_ref[...] = grad
    out.append(copies.start(grad_ref, grad_hbm))
    for r in range(relations):
        at = slice(r * rows, (r + 1) * rows)
        spread = dot(grad, w[r]) * wide(norm[at, :], width)
        spreads[at, :] = spread.astype(bf16)
    slots = packed.shape[0]
    first = local.astype(bf16).astype(f32)
    second = (local - first).astype(bf16).astype(f32)
    third = local - first - second
    lane = iota((slots, EXTRA), 1)
    packed[:, width:] = jnp.where(lane < 32, first, jnp.where(lane < 64, second, third)).astype(bf16)
    back_in.wait()
    packed[:, :width] = dot(back[rows:, :], spreads[...]).astype(bf16)
    out.append(copies.start(packed, out_hbm))
    local_ref[...] = dot(back[:rows, :], spreads[...]) + dot(grad, selfs[...])
    out.append(copies.start(local_ref, local_hbm))
    wait_all(out)


def turn_kernel(block, me_ref, left_hbm, keep_hbm, send_hbm, left, turned, blocks, sems):
    copies = Copies(sems)
    step = turned.shape[0] // 3
    cuts = [slice(i * step, (i + 1) * step) for i in range(3)]
    ins = [copies.start(left_hbm.at[:, at], left.at[:, at]) for at in cuts]
    for at, copy in zip(cuts, ins):
        copy.wait()
        turned[at, :] = left[:, at].T.astype(turned.dtype)
    put_blocks(me_ref[0], turned, blocks, block)
    wait_all([copies.start(blocks.at[0], keep_hbm), copies.start(blocks.at[1], send_hbm)])


def grad_pre_kernel(
    got_ref, local_ref, after_ref, picks_hbm, count_hbm, hid_hbm, total_hbm, out_ref, loss_ref,
    picks, counts, hid, total, sems,
):
    copies = Copies(sems)
    pairs = ((picks_hbm, picks), (count_hbm, counts), (hid_hbm, hid), (total_hbm, total))
    wait_all([copies.start(a, b) for a, b in pairs])
    rows, width = hid.shape
    grad = local_ref[...] + dot(pick_hot(picks[...], counts[...], rows), got_ref[:, :width])
    out_ref[...] = jnp.where(hid[...].astype(f32) > 0.0, grad, 0.0).astype(bf16)
    sums = jnp.sum(got_ref[:, width:].astype(f32), axis=0, keepdims=True)
    loss = (sums[:, 0:1] + sums[:, 32:33] + sums[:, 64:65]) * 0.125
    loss_ref[...] = loss / total[0:1, 0:1]


class Colour:
    def __init__(self, start, size, order):
        self.start, self.size, self.order = start, size, order

    def places(self, stage):
        gone = self.order[:stage]
        bits = len(self.order)
        return [p for p in range(1 << bits) if not any(p >> g & 1 for g in gone)]

    def split(self, stage):
        bit = self.order[stage]
        here = self.places(stage)
        return [p for p in here if p >> bit & 1], [p for p in here if not p >> bit & 1]


def colours_of(bits, rows):
    tiles = rows // 16
    last = list(range(4, bits))
    orders = [[0, 2, 1, 3] + last, [1, 0, 2, 3] + last, [2, 1, 3, 0] + last]
    third = tiles // 3
    sizes = [tiles - 2 * third, third, third]
    out, at = [], 0
    for size, order in zip(sizes, orders):
        if size:
            out.append(Colour(at * 16, size * 16, order))
        at += size
    return out


def product_kernel(colours, keep_hbm, other_hbm, grad_ref, other_grad_ref, *refs):
    outs, (keep, other, sems) = refs[: 2 * len(colours)], refs[2 * len(colours) :]
    copies = Copies(sems)
    ins = []
    for colour in colours:
        rows = slice(colour.start, colour.start + colour.size)
        ins.append(copies.start(keep_hbm.at[:, rows, :], keep.at[:, rows, :]))
        ins.append(copies.start(other_hbm.at[:, rows, :], other.at[:, rows, :]))
    grad, other_grad = grad_ref[...], other_grad_ref[...]
    width = grad.shape[1]
    for i, colour in enumerate(colours):
        rows = slice(colour.start, colour.start + colour.size)
        wait_all(ins[2 * i : 2 * i + 2])
        for places, out in zip(colour.split(0), outs[2 * i : 2 * i + 2]):
            left = jnp.concatenate([keep[p, rows, :] for p in places], axis=0)
            right = jnp.concatenate([other[p, rows, :] for p in places], axis=0)
            value = dot(left, grad) + dot(right, other_grad)
            out[...] = value.astype(out.dtype).reshape(len(places), colour.size, width)


def add_kernel(colour, stage, got, kept, *outs):
    here = colour.places(stage)
    for places, out in zip(colour.split(stage), outs):
        for j, p in enumerate(places):
            k = here.index(p)
            out[j] = (kept[k] + got[k].astype(f32)).astype(out.dtype)


def last_kernel(colours, block, *refs):
    out = refs[-1]
    for i, colour in enumerate(colours):
        got, kept = refs[2 * i], refs[2 * i + 1]
        size = min(colour.size, block - colour.start)
        if size > 0:
            value = kept[0] + got[0].astype(f32)
            out[colour.start : colour.start + size, :] = value[:size]


def across(value, bit):
    size = lax.axis_size("dom")
    return lax.ppermute(value, "dom", [(i, i ^ (2 << bit)) for i in range(size)])


def to_pair(value):
    size = lax.axis_size("dom")
    return lax.ppermute(value, "dom", [(i, i ^ 1) for i in range(size)])


def product(colours, keep, other, grad, other_grad):
    width = grad.shape[1]
    outs = []
    for colour in colours:
        sent, kept = colour.split(0)
        outs.append(((len(sent), colour.size, width), bf16))
        outs.append(((len(kept), colour.size, width), f32))
    ins = (keep, other, grad, other_grad)
    return call(
        functools.partial(product_kernel, colours), outs, ins, "hhvv", "v" * len(outs),
        [pltpu.VMEM(keep.shape, bf16)] * 2, 2 * len(colours),
        flops=4 * keep.size * width, moved=keep.size * 12, vmem=16,
    )


def add_stage(colour, stage, got, kept):
    sent, keep = colour.split(stage)
    outs = [((len(sent),) + got.shape[1:], bf16), ((len(keep),) + got.shape[1:], f32)]
    return call(
        functools.partial(add_kernel, colour, stage), outs, (got, kept), "vv", "vv",
        flops=got.size * 200, moved=got.size * 10, vmem=4,
    )


def scatter_sum(colours, block, parts):
    bits = len(colours[0].order)
    ends = []
    states = [list(parts[2 * i : 2 * i + 2]) for i in range(len(colours))]
    for stage in range(bits):
        for i, colour in enumerate(colours):
            sent, kept = states[i]
            got = across(sent, colour.order[stage])
            if stage + 1 < bits:
                states[i] = add_stage(colour, stage + 1, got, kept)
            else:
                ends += [got, kept]
    return call(
        functools.partial(last_kernel, colours, block), [((block, ends[0].shape[2]), f32)], ends,
        "v" * len(ends), "v", flops=block * 1000, moved=block * 5000, vmem=4,
    )[0]


def exchange(value):
    peers = lax.axis_size("dom")
    slots = value.shape[0] // peers
    cut = value.reshape(peers, slots, value.shape[1])
    got = lax.all_to_all(cut, "dom", split_axis=0, concat_axis=0, tiled=True)
    return got.reshape(value.shape)


def on_device(features, w_one, w_two, self_two, edge_src, edge_dst, send_rows, send_count, labels):
    peers = lax.axis_size("dom")
    rows, width = features.shape
    relations, _, classes = w_two.shape
    blocks, edges = edge_src.shape[1:]
    picks = send_rows[0].T
    slots = picks.shape[0]
    boundary = peers * slots
    table = rows + boundary
    label_row = labels.reshape(1, rows)
    me = lax.axis_index("dom").astype(jnp.int32).reshape(1)
    all_rows = relations * rows
    block = (relations + 1) * width // peers
    padded = -(-block // 16) * 16
    bits = peers.bit_length() - 2
    colours = colours_of(bits, padded)
    w_two = jnp.swapaxes(w_two, 1, 2)
    self_two = self_two.T

    vm = pltpu.VMEM
    picks_vm, counts_vm = vm((slots, peers), jnp.int32), vm((1, peers), jnp.int32)
    own_vm, total_vm = vm((rows, width), bf16), vm((8, EXTRA), f32)
    adj_vm, norm_vm = vm((all_rows, table), bf16), vm((all_rows, EXTRA), f32)
    back_vm = vm((table, all_rows), bf16)
    edge_vm = vm((relations, blocks, edges), jnp.int32)
    deep = (relations + 1) * width
    left_vm = vm((rows, deep), bf16)
    turned_vm = vm((deep, rows), bf16 if block % 16 == 0 else f32)
    blocks_vm = vm((2, peers // 2, padded, rows), bf16)
    turn_outs = [((peers // 2, padded, rows), bf16)] * 2
    packed_vm = vm((boundary, width + EXTRA), bf16)

    packed, = call(
        pack_kernel, [((boundary, width + EXTRA), bf16)], (features, picks, send_count, label_row),
        "hhhh", "v", [own_vm, picks_vm, counts_vm, vm((1, rows), jnp.int32)], 4,
        flops=2 * boundary * rows * width, moved=600000,
    )
    got_one = exchange(packed)
    adj, norm, back = call(
        graph_kernel,
        [((all_rows, table), bf16), ((all_rows, EXTRA), f32), ((table, all_rows), bf16)],
        (edge_src, edge_dst), "hh", "hhh", [edge_vm] * 2 + [adj_vm, norm_vm, back_vm], 5,
        flops=4 * all_rows * 256 * table, moved=5 << 20,
    )
    left_one, hidden, packed, total = call(
        first_kernel,
        [((rows, deep), bf16), ((rows, width), bf16), ((boundary, width), bf16), ((8, EXTRA), f32)],
        (adj, norm, got_one, features, w_one.reshape(deep, width), picks, send_count), "hhhhhhh", "hhhh",
        [
            adj_vm, norm_vm, packed_vm, own_vm, vm((deep, width), bf16), picks_vm, counts_vm, left_vm,
            own_vm, vm((boundary, width), bf16), total_vm,
        ],
        7 + relations + 4,
        flops=2 * all_rows * width * (table + width), moved=10 << 20,
    )
    got_two = exchange(packed)
    keep_one, send_one = call(
        functools.partial(turn_kernel, block), turn_outs, (me, left_one), "sh", "hh",
        [left_vm, turned_vm, blocks_vm], 5, flops=1 << 30, moved=5 << 20,
    )
    other_one = to_pair(send_one)
    logits, keep_two, send_two, grad_logits, local, outgoing = call(
        functools.partial(second_kernel, block),
        [((classes, rows), f32)] + turn_outs
        + [((rows, classes), bf16), ((rows, width), f32), ((boundary, width + EXTRA), bf16)],
        (me, got_two, adj, norm, back, hidden, w_two, self_two, label_row, total), "shhhhhhhhh", "hhhhhh",
        [
            vm((boundary, width), bf16), adj_vm, norm_vm, back_vm, own_vm, vm(w_two.shape, bf16),
            vm(self_two.shape, bf16), vm((1, rows), jnp.int32), total_vm, vm((classes, rows), f32),
            turned_vm, blocks_vm, vm((rows, classes), bf16), vm((all_rows, width), bf16),
            vm((rows, width), f32), packed_vm,
        ],
        2 + 3 * (relations // 2) + 4 + 6,
        flops=8 * all_rows * width * width, moved=16 << 20,
    )
    other_two, other_logits = to_pair(send_two), to_pair(grad_logits)
    returned = exchange(outgoing)
    parts_two = product(colours, keep_two, other_two, grad_logits, other_logits)
    grad_pre, loss = call(
        grad_pre_kernel, [((rows, width), bf16), ((1, 1), f32)],
        (returned, local, parts_two[0], picks, send_count, hidden, total), "vvhhhhh", "vv",
        [picks_vm, counts_vm, own_vm, total_vm], 4,
        flops=2 * rows * boundary * width, moved=2 << 20, vmem=50,
    )
    other_pre = to_pair(grad_pre)
    parts_one = product(colours, keep_one, other_one, grad_pre, other_pre)
    grad_two = scatter_sum(colours, block, parts_two)
    grad_one = scatter_sum(colours, block, parts_one)
    return (logits.T, loss.reshape(()), grad_one, grad_two)


def solution(mesh):
    in_specs = (
        P("dom", None),
        P(),
        P(),
        P(),
        P(None, "dom", None),
        P(None, "dom", None),
        P("dom", None, None),
        P("dom", None),
        P("dom"),
    )
    out_specs = (P("dom", None), P(), P("dom", None), P("dom", None))
    return jax.shard_map(on_device, mesh=mesh, in_specs=in_specs, out_specs=out_specs, check_vma=False)
```

profile of v0, /device:TPU:0, one launch (start us, length us, event | category | flops | bytes accessed | tf_op | source)
XLA Modules:
  0.0 127.0 jit_solution(3633383498543033877)
XLA Ops:
  0.6 2.2 %shard_map.121 = bf16[256,640]{1,0:T(8,128)(2,1)} custom-call(bf16[256,512]{1,0:T(8,128)(2,1)} %feat_hbm.3, s32[8,32]{1,0:T(8,128)} %bitcast.19, s32[1,32]{1,0:T(1,128)} %count_hbm.5, s32[1,256]{1,0:T(1,128)} %bitcast.27), custom_call_target="tpu_custom_call" | custom-call | flops 67108864 | bytes 600000 | tf_op jit(solution)/shard_map/pallas_call | solution.py:43
  2.8 7.4 %all-to-all-start = ((bf16[32,8,640]{2,1,0:T(8,128)(2,1)}), bf16[32,8,640]{2,1,0:T(8,128)(2,1)}, u32[]{:S(2)}, u32[]{:S(2)}) async-start(bf16[32,8,640]{2,1,0:T(8,128)(2,1)} %bitcast.24), calls=%async_computation | async-start | bytes 655360 | tf_op jit(solution)/shard_map/all_to_all | solution.py:409
  10.3 6.7 %shard_map.120 = (bf16[2048,512]{1,0:T(8,128)(2,1)}, f32[2048,128]{1,0:T(8,128)}, bf16[512,2048]{1,0:T(8,128)(2,1)}) custom-call(s32[8,2,256]{2,1,0:T(2,128)} %src_hbm.1, s32[8,2,256]{2,1,0:T(2,128)} %dst_hbm.1), custom_call_target="tpu_custom_call" | custom-call | flops 1073741824 | bytes 5242880 | tf_op jit(solution)/shard_map/pallas_call | solution.py:43
  16.9 5.4 %all-to-all-done = bf16[32,8,640]{2,1,0:T(8,128)(2,1)} async-done(((bf16[32,8,640]{2,1,0:T(8,128)(2,1)}), bf16[32,8,640]{2,1,0:T(8,128)(2,1)}, u32[]{:S(2)}, u32[]{:S(2)}) %all-to-all-start) | async-done | bytes 327712 | tf_op jit(solution)/shard_map/all_to_all | solution.py:409
  22.3 6.2 %shard_map.122 = (bf16[256,4608]{1,0:T(8,128)(2,1)}, bf16[256,512]{1,0:T(8,128)(2,1)}, bf16[256,512]{1,0:T(8,128)(2,1)}, f32[8,128]{1,0:T(8,128)}) custom-call(bf16[2048,512]{1,0:T(8,128)(2,1)} %get-tuple-element.69.adj_hbm, f32[2048,128]{1,0:T(8,128)} %get-tuple-element.70.norm_hbm, bf16[256,640]{1,0:T(8,128)(2,1)} %bitcast.5.got_hbm, ...), custom_call_target="tpu_custom_call" | custom-call | flops 2147483648 | bytes 10485760 | tf_op jit(solution)/shard_map/pallas_call | solution.py:43
  28.5 3.3 %all-to-all-start.1 = ((bf16[32,8,512]{2,1,0:T(8,128)(2,1)}), bf16[32,8,512]{2,1,0:T(8,128)(2,1)}, u32[]{:S(2)}, u32[]{:S(2)}) async-start(bf16[32,8,512]{2,1,0:T(8,128)(2,1)} %bitcast.26), calls=%async_computation.1 | async-start | bytes 524288 | tf_op jit(solution)/shard_map/all_to_all | solution.py:409
  31.9 4.3 %copy.15 = bf16[8,512,349]{1,2,0:T(8,128)(2,1)} copy(bf16[8,512,349]{1,0,2:T(8,128)(2,1)} %param.11) | data formatting | bytes 5718016 | tf_op args[2]
  36.1 6.3 %all-to-all-done.1 = bf16[32,8,512]{2,1,0:T(8,128)(2,1)} async-done(((bf16[32,8,512]{2,1,0:T(8,128)(2,1)}), bf16[32,8,512]{2,1,0:T(8,128)(2,1)}, u32[]{:S(2)}, u32[]{:S(2)}) %all-to-all-start.1) | async-done | bytes 262176 | tf_op jit(solution)/shard_map/all_to_all | solution.py:409
  42.4 9.9 %shard_map.123 = (f32[349,256]{1,0:T(8,128)}, bf16[16,144,256]{2,1,0:T(8,128)(2,1)}, bf16[16,144,256]{2,1,0:T(8,128)(2,1)}, bf16[256,349]{1,0:T(8,128)(2,1)}, f3...) custom-call(s32[1]{0:T(128)} %bitcast.me_ref, bf16[256,512]{1,0:T(8,128)(2,1)} %bitcast.8.got_hbm, ...), custom_call_target="tpu_custom_call" | custom-call | flops 4294967296 | bytes 16777216 | tf_op jit(solution)/shard_map/pallas_call | solution.py:43
  52.3 0.1 collective-permute-start
  52.4 3.4 %shard_map.126 = (bf16[16,144,256]{2,1,0:T(8,128)(2,1)}, bf16[16,144,256]{2,1,0:T(8,128)(2,1)}) custom-call(s32[1]{0:T(128)} %bitcast.me_ref, bf16[256,4608]{1,0:T(8,128)(2,1)} %get-tuple-element.83.left_hbm), custom_call_target="tpu_custom_call" | custom-call | flops 1073741824 | bytes 5242880 | tf_op jit(solution)/shard_map/pallas_call | solution.py:43
  55.9 0.6 collective-permute-start.2
  56.4 2.8 %all-to-all-start.2 = ((bf16[32,8,640]{2,1,0:T(8,128)(2,1)}), bf16[32,8,640]{2,1,0:T(8,128)(2,1)S(1)}, u32[]{:S(2)}, u32[]{:S(2)}) async-start(bf16[32,8,640]{2,1,0:T(8,128)(2,1)} %bitcast.25), calls=%async_computation.2 | async-start | bytes 655360 | tf_op jit(solution)/shard_map/all_to_all | solution.py:409
  59.2 0.1 collective-permute-start.1
  59.3 1.6 %collective-permute-done.1.other_grad_ref = bf16[256,349]{1,0:T(8,128)(2,1)S(1)} collective-permute-done((bf16[256,349]{1,0:T(8,128)(2,1)}, bf16[256,349]{1,0:T(8,128)(2,1)S(1)}, u32[]{:S(2)}, u32[]{:S(2)}) %collective-permute-start.1) | collective-permute-done | bytes 178720 | tf_op jit(solution)/shard_map/ppermute | solution.py:360
  60.9 0.9 copy-done.6
  61.9 1.3 copy-done.7
  63.1 2.8 %shard_map.124 = (bf16[8,48,349]{2,1,0:T(8,128)(2,1)S(1)}, f32[8,48,349]{2,1,0:T(8,128)S(1)}, bf16[8,48,349]{2,1,0:T(8,128)(2,1)S(1)}, f32[8,48,349]{2,1,0:T(8,1...) custom-call(bf16[16,144,256]{2,1,0:T(8,128)(2,1)S(1)} %copy-done.7, ...), custom_call_target="tpu_custom_call" | custom-call | flops 823394304 | bytes 7077888 | tf_op jit(solution)/shard_map/pallas_call | solution.py:43
  66.0 0.7 copy-done.5
  66.7 4.4 %all-to-all-done.2 = bf16[32,8,640]{2,1,0:T(8,128)(2,1)S(1)} async-done(((bf16[32,8,640]{2,1,0:T(8,128)(2,1)}), bf16[32,8,640]{2,1,0:T(8,128)(2,1)S(1)}, u32[]{:S(2)}, u32[]{:S(2)}) %all-to-all-start.2) | async-done | bytes 327712 | tf_op jit(solution)/shard_map/all_to_all | solution.py:409
  71.1 0.9 shard_map.125
  72.0 0.1 collective-permute-start.3
  72.1 0.8 collective-permute-start.20
  72.9 0.7 collective-permute-done.3.other_grad_ref
  73.6 1.3 copy-done.8
  74.9 2.8 %shard_map.127 = (bf16[8,48,512]{2,1,0:T(8,128)(2,1)S(1)}, f32[8,48,512]{2,1,0:T(8,128)S(1)}, bf16[8,48,512]{2,1,0:T(8,128)(2,1)S(1)}, f32[8,48,512]{2,1,0:T(8,1...) custom-call(bf16[16,144,256]{2,1,0:T(8,128)(2,1)S(1)} %copy-done.8, ...), custom_call_target="tpu_custom_call" | custom-call | flops 1207959552 | bytes 7077888 | tf_op jit(solution)/shard_map/pallas_call | solution.py:43
  77.7 0.4 collective-permute-start.4
  78.1 1.3 %collective-permute-start.8 = (bf16[8,48,512]{2,1,0:T(8,128)(2,1)S(1)}, bf16[8,48,512]{2,1,0:T(8,128)(2,1)S(1)}, u32[]{:S(2)}, u32[]{:S(2)}) collective-permute-start(bf16[8,48,512]{2,1,0:T(8,128)(2,1)S(1)} %get-tuple-element.95), channel_id=1, source_target_pairs={{0,4},{1,5},{2,6},{3,7},{4,0},{5,1},{6,2},{7,3},{8,12},{9,13},{10,... | collective-permute-start | bytes 1179656 | tf_op jit(solution)/shard_map/ppermute | solution.py:355
  79.5 0.3 collective-permute-start.12
  79.8 1.7 %collective-permute-start.24 = (bf16[8,48,349]{2,1,0:T(8,128)(2,1)S(1)}, bf16[8,48,349]{2,1,0:T(8,128)(2,1)S(1)}, u32[]{:S(2)}, u32[]{:S(2)}) collective-permute-start(bf16[8,48,349]{2,1,0:T(8,128)(2,1)S(1)} %get-tuple-element.126), channel_id=1, source_target_pairs={{0,8},{1,9},{2,10},{3,11},{4,12},{5,13},{6,14},{7,15},{8,0},{9,1},... | collective-permute-start | bytes 804104 | tf_op jit(solution)/shard_map/ppermute | solution.py:355
  81.5 0.8 collective-permute-done.20.got
  82.3 0.3 collective-permute-start.16
  82.6 7.1 %collective-permute-done.4.got = bf16[8,48,512]{2,1,0:T(8,128)(2,1)S(1)} collective-permute-done((bf16[8,48,512]{2,1,0:T(8,128)(2,1)S(1)}, bf16[8,48,512]{2,1,0:T(8,128)(2,1)S(1)}, u32[]{:S(2)}, u32[]{:S(2)}) %collective-permute-start.4) | collective-permute-done | bytes 393248 | tf_op jit(solution)/shard_map/ppermute | solution.py:355
  89.8 0.3 collective-permute-start.21
  90.1 0.1 shard_map.128
  90.2 0.8 collective-permute-start.5
  91.0 0.1 shard_map.131
  91.0 0.4 collective-permute-done.12.got
  91.4 1.4 %collective-permute-start.9 = (bf16[4,48,512]{2,1,0:T(8,128)(2,1)S(1)}, bf16[4,48,512]{2,1,0:T(8,128)(2,1)S(1)}, u32[]{:S(2)}, u32[]{:S(2)}) collective-permute-start(bf16[4,48,512]{2,1,0:T(8,128)(2,1)S(1)} %get-tuple-element.97), channel_id=1, source_target_pairs={{0,2},{1,3},{2,0},{3,1},{4,6},{5,7},{6,4},{7,5},{8,10},{9,11},{10,... | collective-permute-start | bytes 589832 | tf_op jit(solution)/shard_map/ppermute | solution.py:355
  92.9 0.1 shard_map.134
  92.9 4.8 %collective-permute-done.24.got = bf16[8,48,349]{2,1,0:T(8,128)(2,1)S(1)} collective-permute-done((bf16[8,48,349]{2,1,0:T(8,128)(2,1)S(1)}, bf16[8,48,349]{2,1,0:T(8,128)(2,1)S(1)}, u32[]{:S(2)}, u32[]{:S(2)}) %collective-permute-start.24) | collective-permute-done | bytes 268064 | tf_op jit(solution)/shard_map/ppermute | solution.py:355
  97.8 0.7 collective-permute-start.13
  98.5 1.4 %collective-permute-start.25 = (bf16[4,48,349]{2,1,0:T(8,128)(2,1)S(1)}, bf16[4,48,349]{2,1,0:T(8,128)(2,1)S(1)}, u32[]{:S(2)}, u32[]{:S(2)}) collective-permute-start(bf16[4,48,349]{2,1,0:T(8,128)(2,1)S(1)} %get-tuple-element.128), channel_id=1, source_target_pairs={{0,4},{1,5},{2,6},{3,7},{4,0},{5,1},{6,2},{7,3},{8,12},{9,13},{10,... | collective-permute-start | bytes 402056 | tf_op jit(solution)/shard_map/ppermute | solution.py:355
  100.0 0.4 collective-permute-start.17
  100.4 0.5 collective-permute-done.5.got
  100.9 1.3 %collective-permute-start.22 = (bf16[2,48,349]{2,1,0:T(8,128)(2,1)S(1)}, bf16[2,48,349]{2,1,0:T(8,128)(2,1)S(1)}, u32[]{:S(2)}, u32[]{:S(2)}) collective-permute-start(bf16[2,48,349]{2,1,0:T(8,128)(2,1)S(1)} %get-tuple-element.122), channel_id=1, source_target_pairs={{0,8},{1,9},{2,10},{3,11},{4,12},{5,13},{6,14},{7,15},{8,0},{9,1},... | collective-permute-start | bytes 201032 | tf_op jit(solution)/shard_map/ppermute | solution.py:355
  102.2 0.4 collective-permute-done.9.got
  102.6 0.8 collective-permute-start.6
  103.4 0.1 collective-permute-done.13.got
  103.5 0.8 collective-permute-start.10
  104.3 1.3 %collective-permute-done.25.got = bf16[4,48,349]{2,1,0:T(8,128)(2,1)S(1)} collective-permute-done((bf16[4,48,349]{2,1,0:T(8,128)(2,1)S(1)}, bf16[4,48,349]{2,1,0:T(8,128)(2,1)S(1)}, u32[]{:S(2)}, u32[]{:S(2)}) %collective-permute-start.25) | collective-permute-done | bytes 134048 | tf_op jit(solution)/shard_map/ppermute | solution.py:355
  105.7 3.0 %collective-permute-start.26 = (bf16[2,48,349]{2,1,0:T(8,128)(2,1)S(1)}, bf16[2,48,349]{2,1,0:T(8,128)(2,1)S(1)}, u32[]{:S(2)}, u32[]{:S(2)}) collective-permute-start(bf16[2,48,349]{2,1,0:T(8,128)(2,1)S(1)} %get-tuple-element.130), channel_id=1, source_target_pairs={{0,16},{1,17},{2,18},{3,19},{4,20},{5,21},{6,22},{7,23},{8,24},{9,... | collective-permute-start | bytes 201032 | tf_op jit(solution)/shard_map/ppermute | solution.py:355
  108.7 1.6 %collective-permute-start.18 = (bf16[2,48,349]{2,1,0:T(8,128)(2,1)S(1)}, bf16[2,48,349]{2,1,0:T(8,128)(2,1)S(1)}, u32[]{:S(2)}, u32[]{:S(2)}) collective-permute-start(bf16[2,48,349]{2,1,0:T(8,128)(2,1)S(1)} %get-tuple-element.114), channel_id=1, source_target_pairs={{0,4},{1,5},{2,6},{3,7},{4,0},{5,1},{6,2},{7,3},{8,12},{9,13},{10,... | collective-permute-start | bytes 201032 | tf_op jit(solution)/shard_map/ppermute | solution.py:355
  110.4 0.3 collective-permute-start.23
  110.7 2.7 %collective-permute-start.7 = (bf16[1,48,512]{2,1,0:T(8,128)(2,1)S(1)}, bf16[1,48,512]{2,1,0:T(8,128)(2,1)S(1)}, u32[]{:S(2)}, u32[]{:S(2)}) collective-permute-start(bf16[1,48,512]{2,1,0:T(8,128)(2,1)S(1)} %get-tuple-element.93), channel_id=1, source_target_pairs={{0,16},{1,17},{2,18},{3,19},{4,20},{5,21},{6,22},{7,23},{8,24},{9,... | collective-permute-start | bytes 147464 | tf_op jit(solution)/shard_map/ppermute | solution.py:355
  113.5 2.3 %collective-permute-done.14.got = bf16[2,48,512]{2,1,0:T(8,128)(2,1)S(1)} collective-permute-done((bf16[2,48,512]{2,1,0:T(8,128)(2,1)S(1)}, bf16[2,48,512]{2,1,0:T(8,128)(2,1)S(1)}, u32[]{:S(2)}, u32[]{:S(2)}) %collective-permute-start.14) | collective-permute-done | bytes 98336 | tf_op jit(solution)/shard_map/ppermute | solution.py:355
  115.8 2.3 %collective-permute-done.26.got = bf16[2,48,349]{2,1,0:T(8,128)(2,1)S(1)} collective-permute-done((bf16[2,48,349]{2,1,0:T(8,128)(2,1)S(1)}, bf16[2,48,349]{2,1,0:T(8,128)(2,1)S(1)}, u32[]{:S(2)}, u32[]{:S(2)}) %collective-permute-start.26) | collective-permute-done | bytes 67040 | tf_op jit(solution)/shard_map/ppermute | solution.py:355
  118.1 0.5 collective-permute-start.15
  118.6 1.6 %collective-permute-start.27 = (bf16[1,48,349]{2,1,0:T(8,128)(2,1)S(1)}, bf16[1,48,349]{2,1,0:T(8,128)(2,1)S(1)}, u32[]{:S(2)}, u32[]{:S(2)}) collective-permute-start(bf16[1,48,349]{2,1,0:T(8,128)(2,1)S(1)} %get-tuple-element.132), channel_id=1, source_target_pairs={{0,2},{1,3},{2,0},{3,1},{4,6},{5,7},{6,4},{7,5},{8,10},{9,11},{10,... | collective-permute-start | bytes 100520 | tf_op jit(solution)/shard_map/ppermute | solution.py:355
  120.2 0.8 collective-permute-start.19
  121.0 1.7 %collective-permute-done.27.refs_4_ = bf16[1,48,349]{2,1,0:T(8,128)(2,1)S(1)} collective-permute-done((bf16[1,48,349]{2,1,0:T(8,128)(2,1)S(1)}, bf16[1,48,349]{2,1,0:T(8,128)(2,1)S(1)}, u32[]{:S(2)}, u32[]{:S(2)}) %collective-permute-start.27) | collective-permute-done | bytes 33536 | tf_op jit(solution)/shard_map/ppermute | solution.py:355
  122.7 2.9 %collective-permute-done.19.refs_0_ = bf16[1,48,349]{2,1,0:T(8,128)(2,1)S(1)} collective-permute-done((bf16[1,48,349]{2,1,0:T(8,128)(2,1)S(1)}, bf16[1,48,349]{2,1,0:T(8,128)(2,1)S(1)}, u32[]{:S(2)}, u32[]{:S(2)}) %collective-permute-start.19) | collective-permute-done | bytes 33536 | tf_op jit(solution)/shard_map/ppermute | solution.py:355
  125.6 0.7 shard_map.147
  126.3 0.7 shard_map.137
  (45 shorter events, 0.5 us)
Async XLA Ops:
  2.8 19.5 %all-to-all-start = ((bf16[32,8,640]{2,1,0:T(8,128)(2,1)}), bf16[32,8,640]{2,1,0:T(8,128)(2,1)}, u32[]{:S(2)}, u32[]{:S(2)}) async-start(bf16[32,8,640]{2,1,0:T(8,128)(2,1)} %bitcast.24), calls=%async_computation | async-start | bytes 655360 | tf_op jit(solution)/shard_map/all_to_all | solution.py:409
  28.5 13.9 %all-to-all-start.1 = ((bf16[32,8,512]{2,1,0:T(8,128)(2,1)}), bf16[32,8,512]{2,1,0:T(8,128)(2,1)}, u32[]{:S(2)}, u32[]{:S(2)}) async-start(bf16[32,8,512]{2,1,0:T(8,128)(2,1)} %bitcast.26), calls=%async_computation.1 | async-start | bytes 524288 | tf_op jit(solution)/shard_map/all_to_all | solution.py:409
  52.3 8.6 %collective-permute-start = (bf16[16,144,256]{2,1,0:T(8,128)(2,1)}, bf16[16,144,256]{2,1,0:T(8,128)(2,1)}, u32[]{:S(2)}, u32[]{:S(2)}) collective-permute-start(bf16[16,144,256]{2,1,0:T(8,128)(2,1)} %get-tuple-element.79), channel_id=1, source_target_pairs={{0,1},{1,0},{2,3},{3,2},{4,5},{5,4},{6,7},{7,6},{8,9},{9,8},{10,11... | collective-permute-start | bytes 3538952 | tf_op jit(solution)/shard_map/ppermute | solution.py:360
  55.8 15.3 %copy-start = (f32[256,512]{1,0:T(8,128)S(1)}, f32[256,512]{1,0:T(8,128)}, u32[]{:S(2)}) copy-start(f32[256,512]{1,0:T(8,128)} %get-tuple-element.77.local_ref) | copy-start | bytes 1572868
  55.8 15.2 %copy-start.1 = (bf16[256,512]{1,0:T(8,128)(2,1)S(1)}, bf16[256,512]{1,0:T(8,128)(2,1)}, u32[]{:S(2)}) copy-start(bf16[256,512]{1,0:T(8,128)(2,1)} %get-tuple-element.73.hid_hbm) | copy-start | bytes 786436
  55.9 15.2 %copy-start.2 = (s32[1,32,8]{1,2,0:T(8,128)S(1)}, s32[1,32,8]{1,2,0:T(8,128)}, u32[]{:S(2)}) copy-start(s32[1,32,8]{1,2,0:T(8,128)} %param.15) | copy-start | bytes 3076
  55.9 15.2 %copy-start.3 = (s32[1,32]{1,0:T(1,128)S(1)}, s32[1,32]{1,0:T(1,128)}, u32[]{:S(2)}) copy-start(s32[1,32]{1,0:T(1,128)} %count_hbm.5) | copy-start | bytes 388
  55.9 15.2 %copy-start.4 = (f32[8,128]{1,0:T(8,128)S(1)}, f32[8,128]{1,0:T(8,128)}, u32[]{:S(2)}) copy-start(f32[8,128]{1,0:T(8,128)} %get-tuple-element.74.total_hbm) | copy-start | bytes 12292
  55.9 17.1 %collective-permute-start.2 = (bf16[16,144,256]{2,1,0:T(8,128)(2,1)}, bf16[16,144,256]{2,1,0:T(8,128)(2,1)}, u32[]{:S(2)}, u32[]{:S(2)}) collective-permute-start(bf16[16,144,256]{2,1,0:T(8,128)(2,1)} %get-tuple-element.85), channel_id=1, source_target_pairs={{0,1},{1,0},{2,3},{3,2},{4,5},{5,4},{6,7},{7,6},{8,9},{9,8},{10,11... | collective-permute-start | bytes 3538952 | tf_op jit(solution)/shard_map/ppermute | solution.py:360
  56.4 14.6 %all-to-all-start.2 = ((bf16[32,8,640]{2,1,0:T(8,128)(2,1)}), bf16[32,8,640]{2,1,0:T(8,128)(2,1)S(1)}, u32[]{:S(2)}, u32[]{:S(2)}) async-start(bf16[32,8,640]{2,1,0:T(8,128)(2,1)} %bitcast.25), calls=%async_computation.2 | async-start | bytes 655360 | tf_op jit(solution)/shard_map/all_to_all | solution.py:409
  59.2 1.7 %collective-permute-start.1 = (bf16[256,349]{1,0:T(8,128)(2,1)}, bf16[256,349]{1,0:T(8,128)(2,1)S(1)}, u32[]{:S(2)}, u32[]{:S(2)}) collective-permute-start(bf16[256,349]{1,0:T(8,128)(2,1)} %get-tuple-element.80.grad_ref), channel_id=1, source_target_pairs={{0,1},{1,0},{2,3},{3,2},{4,5},{5,4},{6,7},{7,6},{8,9},{9,8},{10,11... | collective-permute-start | bytes 536072 | tf_op jit(solution)/shard_map/ppermute | solution.py:360
  60.9 0.9 copy-start.6
  61.9 1.3 %copy-start.7 = (bf16[16,144,256]{2,1,0:T(8,128)(2,1)S(1)}, bf16[16,144,256]{2,1,0:T(8,128)(2,1)}, u32[]{:S(2)}) copy-start(bf16[16,144,256]{2,1,0:T(8,128)(2,1)} %get-tuple-element.78.keep_hbm) | copy-start | bytes 3538948
  65.9 0.7 copy-start.5
  72.0 1.6 %collective-permute-start.3 = (bf16[256,512]{1,0:T(8,128)(2,1)S(1)}, bf16[256,512]{1,0:T(8,128)(2,1)S(1)}, u32[]{:S(2)}, u32[]{:S(2)}) collective-permute-start(bf16[256,512]{1,0:T(8,128)(2,1)S(1)} %get-tuple-element.86.grad_ref), channel_id=1, source_target_pairs={{0,1},{1,0},{2,3},{3,2},{4,5},{5,4},{6,7},{7,6},{8,9},{9,8},{10,11... | collective-permute-start | bytes 786440 | tf_op jit(solution)/shard_map/ppermute | solution.py:360
  72.1 10.2 %collective-permute-start.20 = (bf16[8,48,349]{2,1,0:T(8,128)(2,1)}, bf16[8,48,349]{2,1,0:T(8,128)(2,1)S(1)}, u32[]{:S(2)}, u32[]{:S(2)}) collective-permute-start(bf16[8,48,349]{2,1,0:T(8,128)(2,1)} %copy-done.5), channel_id=1, source_target_pairs={{0,4},{1,5},{2,6},{3,7},{4,0},{5,1},{6,2},{7,3},{8,12},{9,13},{10,... | collective-permute-start | bytes 804104 | tf_op jit(solution)/shard_map/ppermute | solution.py:355
  73.6 1.3 %copy-start.8 = (bf16[16,144,256]{2,1,0:T(8,128)(2,1)S(1)}, bf16[16,144,256]{2,1,0:T(8,128)(2,1)}, u32[]{:S(2)}) copy-start(bf16[16,144,256]{2,1,0:T(8,128)(2,1)} %get-tuple-element.84.keep_hbm) | copy-start | bytes 3538948
  77.7 12.1 %collective-permute-start.4 = (bf16[8,48,512]{2,1,0:T(8,128)(2,1)S(1)}, bf16[8,48,512]{2,1,0:T(8,128)(2,1)S(1)}, u32[]{:S(2)}, u32[]{:S(2)}) collective-permute-start(bf16[8,48,512]{2,1,0:T(8,128)(2,1)S(1)} %get-tuple-element.87), channel_id=1, source_target_pairs={{0,2},{1,3},{2,0},{3,1},{4,6},{5,7},{6,4},{7,5},{8,10},{9,11},{10,... | collective-permute-start | bytes 1179656 | tf_op jit(solution)/shard_map/ppermute | solution.py:355
  78.1 12.1 %collective-permute-start.8 = (bf16[8,48,512]{2,1,0:T(8,128)(2,1)S(1)}, bf16[8,48,512]{2,1,0:T(8,128)(2,1)S(1)}, u32[]{:S(2)}, u32[]{:S(2)}) collective-permute-start(bf16[8,48,512]{2,1,0:T(8,128)(2,1)S(1)} %get-tuple-element.95), channel_id=1, source_target_pairs={{0,4},{1,5},{2,6},{3,7},{4,0},{5,1},{6,2},{7,3},{8,12},{9,13},{10,... | collective-permute-start | bytes 1179656 | tf_op jit(solution)/shard_map/ppermute | solution.py:355
  79.5 12.0 %collective-permute-start.12 = (bf16[8,48,512]{2,1,0:T(8,128)(2,1)S(1)}, bf16[8,48,512]{2,1,0:T(8,128)(2,1)S(1)}, u32[]{:S(2)}, u32[]{:S(2)}) collective-permute-start(bf16[8,48,512]{2,1,0:T(8,128)(2,1)S(1)} %get-tuple-element.103), channel_id=1, source_target_pairs={{0,8},{1,9},{2,10},{3,11},{4,12},{5,13},{6,14},{7,15},{8,0},{9,1},... | collective-permute-start | bytes 1179656 | tf_op jit(solution)/shard_map/ppermute | solution.py:355
  79.8 18.0 %collective-permute-start.24 = (bf16[8,48,349]{2,1,0:T(8,128)(2,1)S(1)}, bf16[8,48,349]{2,1,0:T(8,128)(2,1)S(1)}, u32[]{:S(2)}, u32[]{:S(2)}) collective-permute-start(bf16[8,48,349]{2,1,0:T(8,128)(2,1)S(1)} %get-tuple-element.126), channel_id=1, source_target_pairs={{0,8},{1,9},{2,10},{3,11},{4,12},{5,13},{6,14},{7,15},{8,0},{9,1},... | collective-permute-start | bytes 804104 | tf_op jit(solution)/shard_map/ppermute | solution.py:355
  82.3 16.2 %collective-permute-start.16 = (bf16[8,48,349]{2,1,0:T(8,128)(2,1)S(1)}, bf16[8,48,349]{2,1,0:T(8,128)(2,1)S(1)}, u32[]{:S(2)}, u32[]{:S(2)}) collective-permute-start(bf16[8,48,349]{2,1,0:T(8,128)(2,1)S(1)} %get-tuple-element.81.after_ref), channel_id=1, source_target_pairs={{0,2},{1,3},{2,0},{3,1},{4,6},{5,7},{6,4},{7,5},{8,10},{9,11},{10,... | collective-permute-start | bytes 804104 | tf_op jit(solution)/shard_map/ppermute | solution.py:355
  89.8 10.2 %collective-permute-start.21 = (bf16[4,48,349]{2,1,0:T(8,128)(2,1)S(1)}, bf16[4,48,349]{2,1,0:T(8,128)(2,1)S(1)}, u32[]{:S(2)}, u32[]{:S(2)}) collective-permute-start(bf16[4,48,349]{2,1,0:T(8,128)(2,1)S(1)} %get-tuple-element.120), channel_id=1, source_target_pairs={{0,2},{1,3},{2,0},{3,1},{4,6},{5,7},{6,4},{7,5},{8,10},{9,11},{10,... | collective-permute-start | bytes 402056 | tf_op jit(solution)/shard_map/ppermute | solution.py:355
  90.2 10.7 %collective-permute-start.5 = (bf16[4,48,512]{2,1,0:T(8,128)(2,1)S(1)}, bf16[4,48,512]{2,1,0:T(8,128)(2,1)S(1)}, u32[]{:S(2)}, u32[]{:S(2)}) collective-permute-start(bf16[4,48,512]{2,1,0:T(8,128)(2,1)S(1)} %get-tuple-element.89), channel_id=1, source_target_pairs={{0,8},{1,9},{2,10},{3,11},{4,12},{5,13},{6,14},{7,15},{8,0},{9,1},... | collective-permute-start | bytes 589832 | tf_op jit(solution)/shard_map/ppermute | solution.py:355
  91.4 11.2 %collective-permute-start.9 = (bf16[4,48,512]{2,1,0:T(8,128)(2,1)S(1)}, bf16[4,48,512]{2,1,0:T(8,128)(2,1)S(1)}, u32[]{:S(2)}, u32[]{:S(2)}) collective-permute-start(bf16[4,48,512]{2,1,0:T(8,128)(2,1)S(1)} %get-tuple-element.97), channel_id=1, source_target_pairs={{0,2},{1,3},{2,0},{3,1},{4,6},{5,7},{6,4},{7,5},{8,10},{9,11},{10,... | collective-permute-start | bytes 589832 | tf_op jit(solution)/shard_map/ppermute | solution.py:355
  97.8 5.7 %collective-permute-start.13 = (bf16[4,48,512]{2,1,0:T(8,128)(2,1)S(1)}, bf16[4,48,512]{2,1,0:T(8,128)(2,1)S(1)}, u32[]{:S(2)}, u32[]{:S(2)}) collective-permute-start(bf16[4,48,512]{2,1,0:T(8,128)(2,1)S(1)} %get-tuple-element.105), channel_id=1, source_target_pairs={{0,4},{1,5},{2,6},{3,7},{4,0},{5,1},{6,2},{7,3},{8,12},{9,13},{10,... | collective-permute-start | bytes 589832 | tf_op jit(solution)/shard_map/ppermute | solution.py:355
  98.5 7.1 %collective-permute-start.25 = (bf16[4,48,349]{2,1,0:T(8,128)(2,1)S(1)}, bf16[4,48,349]{2,1,0:T(8,128)(2,1)S(1)}, u32[]{:S(2)}, u32[]{:S(2)}) collective-permute-start(bf16[4,48,349]{2,1,0:T(8,128)(2,1)S(1)} %get-tuple-element.128), channel_id=1, source_target_pairs={{0,4},{1,5},{2,6},{3,7},{4,0},{5,1},{6,2},{7,3},{8,12},{9,13},{10,... | collective-permute-start | bytes 402056 | tf_op jit(solution)/shard_map/ppermute | solution.py:355
  100.0 5.7 %collective-permute-start.17 = (bf16[4,48,349]{2,1,0:T(8,128)(2,1)S(1)}, bf16[4,48,349]{2,1,0:T(8,128)(2,1)S(1)}, u32[]{:S(2)}, u32[]{:S(2)}) collective-permute-start(bf16[4,48,349]{2,1,0:T(8,128)(2,1)S(1)} %get-tuple-element.112), channel_id=1, source_target_pairs={{0,8},{1,9},{2,10},{3,11},{4,12},{5,13},{6,14},{7,15},{8,0},{9,1},... | collective-permute-start | bytes 402056 | tf_op jit(solution)/shard_map/ppermute | solution.py:355
  100.9 7.8 %collective-permute-start.22 = (bf16[2,48,349]{2,1,0:T(8,128)(2,1)S(1)}, bf16[2,48,349]{2,1,0:T(8,128)(2,1)S(1)}, u32[]{:S(2)}, u32[]{:S(2)}) collective-permute-start(bf16[2,48,349]{2,1,0:T(8,128)(2,1)S(1)} %get-tuple-element.122), channel_id=1, source_target_pairs={{0,8},{1,9},{2,10},{3,11},{4,12},{5,13},{6,14},{7,15},{8,0},{9,1},... | collective-permute-start | bytes 201032 | tf_op jit(solution)/shard_map/ppermute | solution.py:355
  102.6 7.7 %collective-permute-start.6 = (bf16[2,48,512]{2,1,0:T(8,128)(2,1)S(1)}, bf16[2,48,512]{2,1,0:T(8,128)(2,1)S(1)}, u32[]{:S(2)}, u32[]{:S(2)}) collective-permute-start(bf16[2,48,512]{2,1,0:T(8,128)(2,1)S(1)} %get-tuple-element.91), channel_id=1, source_target_pairs={{0,4},{1,5},{2,6},{3,7},{4,0},{5,1},{6,2},{7,3},{8,12},{9,13},{10,... | collective-permute-start | bytes 294920 | tf_op jit(solution)/shard_map/ppermute | solution.py:355
  103.5 7.2 %collective-permute-start.10 = (bf16[2,48,512]{2,1,0:T(8,128)(2,1)S(1)}, bf16[2,48,512]{2,1,0:T(8,128)(2,1)S(1)}, u32[]{:S(2)}, u32[]{:S(2)}) collective-permute-start(bf16[2,48,512]{2,1,0:T(8,128)(2,1)S(1)} %get-tuple-element.99), channel_id=1, source_target_pairs={{0,8},{1,9},{2,10},{3,11},{4,12},{5,13},{6,14},{7,15},{8,0},{9,1},... | collective-permute-start | bytes 294920 | tf_op jit(solution)/shard_map/ppermute | solution.py:355
  105.6 10.2 %collective-permute-start.14 = (bf16[2,48,512]{2,1,0:T(8,128)(2,1)S(1)}, bf16[2,48,512]{2,1,0:T(8,128)(2,1)S(1)}, u32[]{:S(2)}, u32[]{:S(2)}) collective-permute-start(bf16[2,48,512]{2,1,0:T(8,128)(2,1)S(1)} %get-tuple-element.107), channel_id=1, source_target_pairs={{0,16},{1,17},{2,18},{3,19},{4,20},{5,21},{6,22},{7,23},{8,24},{9,... | collective-permute-start | bytes 294920 | tf_op jit(solution)/shard_map/ppermute | solution.py:355
  105.7 12.4 %collective-permute-start.26 = (bf16[2,48,349]{2,1,0:T(8,128)(2,1)S(1)}, bf16[2,48,349]{2,1,0:T(8,128)(2,1)S(1)}, u32[]{:S(2)}, u32[]{:S(2)}) collective-permute-start(bf16[2,48,349]{2,1,0:T(8,128)(2,1)S(1)} %get-tuple-element.130), channel_id=1, source_target_pairs={{0,16},{1,17},{2,18},{3,19},{4,20},{5,21},{6,22},{7,23},{8,24},{9,... | collective-permute-start | bytes 201032 | tf_op jit(solution)/shard_map/ppermute | solution.py:355
  108.7 9.9 %collective-permute-start.18 = (bf16[2,48,349]{2,1,0:T(8,128)(2,1)S(1)}, bf16[2,48,349]{2,1,0:T(8,128)(2,1)S(1)}, u32[]{:S(2)}, u32[]{:S(2)}) collective-permute-start(bf16[2,48,349]{2,1,0:T(8,128)(2,1)S(1)} %get-tuple-element.114), channel_id=1, source_target_pairs={{0,4},{1,5},{2,6},{3,7},{4,0},{5,1},{6,2},{7,3},{8,12},{9,13},{10,... | collective-permute-start | bytes 201032 | tf_op jit(solution)/shard_map/ppermute | solution.py:355
  110.4 9.9 %collective-permute-start.23 = (bf16[1,48,349]{2,1,0:T(8,128)(2,1)S(1)}, bf16[1,48,349]{2,1,0:T(8,128)(2,1)S(1)}, u32[]{:S(2)}, u32[]{:S(2)}) collective-permute-start(bf16[1,48,349]{2,1,0:T(8,128)(2,1)S(1)} %get-tuple-element.124), channel_id=1, source_target_pairs={{0,16},{1,17},{2,18},{3,19},{4,20},{5,21},{6,22},{7,23},{8,24},{9,... | collective-permute-start | bytes 100520 | tf_op jit(solution)/shard_map/ppermute | solution.py:355
  110.7 15.6 %collective-permute-start.7 = (bf16[1,48,512]{2,1,0:T(8,128)(2,1)S(1)}, bf16[1,48,512]{2,1,0:T(8,128)(2,1)S(1)}, u32[]{:S(2)}, u32[]{:S(2)}) collective-permute-start(bf16[1,48,512]{2,1,0:T(8,128)(2,1)S(1)} %get-tuple-element.93), channel_id=1, source_target_pairs={{0,16},{1,17},{2,18},{3,19},{4,20},{5,21},{6,22},{7,23},{8,24},{9,... | collective-permute-start | bytes 147464 | tf_op jit(solution)/shard_map/ppermute | solution.py:355
  115.8 10.5 %collective-permute-start.11 = (bf16[1,48,512]{2,1,0:T(8,128)(2,1)S(1)}, bf16[1,48,512]{2,1,0:T(8,128)(2,1)S(1)}, u32[]{:S(2)}, u32[]{:S(2)}) collective-permute-start(bf16[1,48,512]{2,1,0:T(8,128)(2,1)S(1)} %get-tuple-element.101), channel_id=1, source_target_pairs={{0,16},{1,17},{2,18},{3,19},{4,20},{5,21},{6,22},{7,23},{8,24},{9,... | collective-permute-start | bytes 147464 | tf_op jit(solution)/shard_map/ppermute | solution.py:355
  118.1 8.2 %collective-permute-start.15 = (bf16[1,48,512]{2,1,0:T(8,128)(2,1)S(1)}, bf16[1,48,512]{2,1,0:T(8,128)(2,1)S(1)}, u32[]{:S(2)}, u32[]{:S(2)}) collective-permute-start(bf16[1,48,512]{2,1,0:T(8,128)(2,1)S(1)} %get-tuple-element.109), channel_id=1, source_target_pairs={{0,2},{1,3},{2,0},{3,1},{4,6},{5,7},{6,4},{7,5},{8,10},{9,11},{10,... | collective-permute-start | bytes 147464 | tf_op jit(solution)/shard_map/ppermute | solution.py:355
  118.6 4.0 %collective-permute-start.27 = (bf16[1,48,349]{2,1,0:T(8,128)(2,1)S(1)}, bf16[1,48,349]{2,1,0:T(8,128)(2,1)S(1)}, u32[]{:S(2)}, u32[]{:S(2)}) collective-permute-start(bf16[1,48,349]{2,1,0:T(8,128)(2,1)S(1)} %get-tuple-element.132), channel_id=1, source_target_pairs={{0,2},{1,3},{2,0},{3,1},{4,6},{5,7},{6,4},{7,5},{8,10},{9,11},{10,... | collective-permute-start | bytes 100520 | tf_op jit(solution)/shard_map/ppermute | solution.py:355
  120.2 5.3 %collective-permute-start.19 = (bf16[1,48,349]{2,1,0:T(8,128)(2,1)S(1)}, bf16[1,48,349]{2,1,0:T(8,128)(2,1)S(1)}, u32[]{:S(2)}, u32[]{:S(2)}) collective-permute-start(bf16[1,48,349]{2,1,0:T(8,128)(2,1)S(1)} %get-tuple-element.116), channel_id=1, source_target_pairs={{0,16},{1,17},{2,18},{3,19},{4,20},{5,21},{6,22},{7,23},{8,24},{9,... | collective-permute-start | bytes 100520 | tf_op jit(solution)/shard_map/ppermute | solution.py:355
where the time goes:
time: 128 us; the launch traced here: 127 us
  waiting for transfers between devices  43 us (34%)
  starting transfers between devices  37.6 us (29%)
  Pallas kernels  37 us (29%)
  local copies, waits for them, and re-layouts  8.49 us (7%)
    pallas_call x28, Pallas kernels, call(): pl.pallas_call(body, out_shape=[jax.ShapeDtypeStruct(s, d) for s, d in ou...  37 us
    ppermute x24, waiting for transfers between devices, across(): return lax.ppermute(value, 'dom', [(i, i ^ 2 << bit) for i in range(size)])  24.6 us
    ppermute x24, starting transfers between devices, across(): return lax.ppermute(value, 'dom', [(i, i ^ 2 << bit) for i in range(size)])  23.2 us
    all_to_all x3, waiting for transfers between devices, exchange(): got = lax.all_to_all(cut, 'dom', split_axis=0, concat_axis=0, tiled=True)  16 us
    all_to_all x3, starting transfers between devices, exchange(): got = lax.all_to_all(cut, 'dom', split_axis=0, concat_axis=0, tiled=True)  13.5 us
    unnamed x19, local copies, waits for them, and re-layouts  8.49 us
  transfers between devices with their start and end apart: 31, of which 17 were waited for; matrix products, arithmetic and copies ran while one was open for 3% of the time, Pallas kernels for 14%

commit v1 on v0

--- a/solution.py
+++ b/solution.py
@@ -30,23 +30,20 @@
     return lax.broadcasted_iota(jnp.int32, shape, axis)
 
 
-HBM = pltpu.HBM
-ALL_VMEM = 67043328
-
-
-def call(body, outs, ins, spaces, out_spaces, scratch=(), copies=0, flops=0, moved=0, vmem=0):
-    kinds = {"v": pltpu.VMEM, "h": pl.ANY, "s": pltpu.SMEM}
-    out_kinds = {"v": pltpu.VMEM, "h": HBM}
+def call(body, outs, ins, spaces, out_spaces, scratch=(), copies=0, flops=0, moved=0, vmem=32):
+    kinds = {"v": pltpu.VMEM, "V": pltpu.VMEM, "H": pltpu.VMEM, "h": pl.ANY, "s": pltpu.SMEM}
+    kept = {"h": pltpu.HBM, "H": pltpu.HBM, "V": pltpu.VMEM}
     scratch = list(scratch)
     if copies:
         scratch.append(pltpu.SemaphoreType.DMA((copies,)))
+    ins = [pltpu.with_memory_space_constraint(x, kept[c]) if c in kept else x for x, c in zip(ins, spaces)]
     return pl.pallas_call(
         body,
-        out_shape=[jax.ShapeDtypeStruct(s, d) for s, d in outs],
+        out_shape=[kept[c](s, d) if c in kept else jax.ShapeDtypeStruct(s, d) for (s, d), c in zip(outs, out_spaces)],
         in_specs=[pl.BlockSpec(memory_space=kinds[c]) for c in spaces],
-        out_specs=[pl.BlockSpec(memory_space=out_kinds[c]) for c in out_spaces],
+        out_specs=[pl.BlockSpec(memory_space=kinds[c]) for c in out_spaces],
         scratch_shapes=scratch,
-        compiler_params=pltpu.CompilerParams(vmem_limit_bytes=vmem << 20 or ALL_VMEM),
+        compiler_params=pltpu.CompilerParams(vmem_limit_bytes=vmem << 20),
         cost_estimate=pl.CostEstimate(flops=flops, bytes_accessed=moved, transcendentals=0),
     )(*ins)
 
@@ -95,7 +92,7 @@
 
 
 def graph_kernel(
-    src_hbm, dst_hbm, adj_hbm, norm_hbm, back_hbm, src_ref, dst_ref, adj_ref, norm_ref, back_ref, sems
+    src_hbm, dst_hbm, adj_ref, norm_ref, back_hbm, src_ref, dst_ref, back_ref, sems
 ):
     copies = Copies(sems)
     wait_all([copies.start(src_hbm, src_ref), copies.start(dst_hbm, dst_ref)])
@@ -118,8 +115,7 @@
         return carry
 
     lax.fori_loop(0, relations, step, 0)
-    pairs = ((adj_ref, adj_hbm), (norm_ref, norm_hbm), (back_ref, back_hbm))
-    wait_all([copies.start(a, b) for a, b in pairs])
+    copies.start(back_ref, back_hbm).wait()
 
 
 def wide(norm, width):
@@ -138,19 +134,16 @@
 
 
 def first_kernel(
-    adj_hbm, norm_hbm, got_hbm, feat_hbm, w_hbm, picks_hbm, count_hbm,
+    adj, norm, got_ref, feat_hbm, w_hbm, picks_hbm, count_hbm,
     left_hbm, hid_hbm, pack_hbm, total_hbm,
-    adj, norm, got_ref, feat, w, picks, counts, left, hid, packed, total_ref, sems,
+    feat, w, picks, counts, left, hid, packed, total_ref, sems,
 ):
     copies = Copies(sems)
     rows, width = feat.shape
     relations = w.shape[0] // width - 1
     chunks = [slice(r * rows, (r + 2) * rows) for r in range(0, relations, 2)]
-    near = [copies.start(feat_hbm, feat), copies.start(got_hbm, got_ref)]
-    adj_in, norm_in, w_in = [], [], []
-    for at in chunks:
-        adj_in.append(copies.start(adj_hbm.at[at, :], adj.at[at, :]))
-        norm_in.append(copies.start(norm_hbm.at[at, :], norm.at[at, :]))
+    near = [copies.start(feat_hbm, feat)]
+    w_in = []
     parts = [slice(0, 4 * width), slice(4 * width, 7 * width), slice(7 * width, (relations + 1) * width)]
     for at in parts:
         w_in.append(copies.start(w_hbm.at[at, :], w.at[at, :]))
@@ -160,8 +153,6 @@
     got = got_ref[:, :width]
     left[:, relations * width :] = own
     for i, at in enumerate(chunks):
-        adj_in[i].wait()
-        norm_in[i].wait()
         sums = dot(adj[at, :rows], own) + dot(adj[at, rows:], got)
         avg = (sums * wide(norm[at, :], width)).astype(bf16)
         left[:, 2 * i * width : (2 * i + 1) * width] = avg[:rows]
@@ -187,20 +178,18 @@
 
 
 def second_kernel(
-    block, me_ref, got_hbm, adj_hbm, norm_hbm, back_hbm, hid_hbm, w_hbm, self_hbm, label_hbm, total_hbm,
+    block, me_ref, got_ref, adj, norm, back_hbm, hid_hbm, w_hbm, self_hbm, label_hbm, total_hbm,
     logit_hbm, keep_hbm, send_hbm, grad_hbm, local_hbm, out_hbm,
-    got_ref, adj, norm, back, hid, w, selfs, label, total, logit, turned, blocks, grad_ref, spreads,
+    back, hid, w, selfs, label, total, logit, turned, blocks, grad_ref, spreads,
     local_ref, packed, sems,
 ):
     copies = Copies(sems)
     rows, width = hid.shape
     relations, classes, _ = w.shape
     chunks = [slice(r * rows, (r + 2) * rows) for r in range(0, relations, 2)]
-    near = [copies.start(hid_hbm, hid), copies.start(got_hbm, got_ref)]
-    adj_in, w_in, norm_in = [], [], []
-    for i, at in enumerate(chunks):
-        adj_in.append(copies.start(adj_hbm.at[at, :], adj.at[at, :]))
-        norm_in.append(copies.start(norm_hbm.at[at, :], norm.at[at, :]))
+    near = [copies.start(hid_hbm, hid)]
+    w_in = []
+    for i in range(len(chunks)):
         w_in.append(copies.start(w_hbm.at[2 * i : 2 * i + 2], w.at[2 * i : 2 * i + 2]))
     small = [copies.start(a, b) for a, b in ((self_hbm, selfs), (label_hbm, label), (total_hbm, total))]
     back_in = copies.start(back_hbm, back)
@@ -210,8 +199,6 @@
     logits = None
     turned[relations * width :, :] = own.T.astype(turned.dtype)
     for i, at in enumerate(chunks):
-        adj_in[i].wait()
-        norm_in[i].wait()
         sums = dot(adj[at, :rows], own) + dot(adj[at, rows:], got)
         avg = (sums * wide(norm[at, :], width)).astype(bf16)
         w_in[i].wait()
@@ -269,18 +256,28 @@
 
 
 def grad_pre_kernel(
-    got_ref, local_ref, after_ref, picks_hbm, count_hbm, hid_hbm, total_hbm, out_ref, loss_ref,
-    picks, counts, hid, total, sems,
+    got_ref, after_ref, local_hbm, hid_hbm, picks_hbm, count_hbm, total_hbm,
+    out_ref, loss_ref, local, hid, picks, counts, total, sems,
 ):
     copies = Copies(sems)
-    pairs = ((picks_hbm, picks), (count_hbm, counts), (hid_hbm, hid), (total_hbm, total))
-    wait_all([copies.start(a, b) for a, b in pairs])
-    rows, width = hid.shape
-    grad = local_ref[...] + dot(pick_hot(picks[...], counts[...], rows), got_ref[:, :width])
-    out_ref[...] = jnp.where(hid[...].astype(f32) > 0.0, grad, 0.0).astype(bf16)
+    pairs = (
+        (picks_hbm, picks), (count_hbm, counts), (local_hbm, local), (hid_hbm, hid), (total_hbm, total),
+    )
+    ins = [copies.start(a, b) for a, b in pairs]
+    wait_all(ins[:2])
+    rows, width = local.shape
+    grad = dot(pick_hot(picks[...], counts[...], rows), got_ref[:, :width])
     sums = jnp.sum(got_ref[:, width:].astype(f32), axis=0, keepdims=True)
     loss = (sums[:, 0:1] + sums[:, 32:33] + sums[:, 64:65]) * 0.125
+    wait_all(ins[2:])
+    out_ref[...] = jnp.where(hid[...].astype(f32) > 0.0, local[...] + grad, 0.0).astype(bf16)
     loss_ref[...] = loss / total[0:1, 0:1]
+
+
+def bring_kernel(*refs):
+    count = len(refs) // 2
+    copies = Copies(refs[-1])
+    wait_all([copies.start(a, b) for a, b in zip(refs[:count], refs[count : 2 * count])])
 
 
 class Colour:
@@ -312,22 +309,14 @@
     return out
 
 
-def product_kernel(colours, keep_hbm, other_hbm, grad_ref, other_grad_ref, *refs):
-    outs, (keep, other, sems) = refs[: 2 * len(colours)], refs[2 * len(colours) :]
-    copies = Copies(sems)
-    ins = []
-    for colour in colours:
-        rows = slice(colour.start, colour.start + colour.size)
-        ins.append(copies.start(keep_hbm.at[:, rows, :], keep.at[:, rows, :]))
-        ins.append(copies.start(other_hbm.at[:, rows, :], other.at[:, rows, :]))
+def product_kernel(colours, keep_ref, other_ref, grad_ref, other_grad_ref, *outs):
     grad, other_grad = grad_ref[...], other_grad_ref[...]
     width = grad.shape[1]
     for i, colour in enumerate(colours):
         rows = slice(colour.start, colour.start + colour.size)
-        wait_all(ins[2 * i : 2 * i + 2])
         for places, out in zip(colour.split(0), outs[2 * i : 2 * i + 2]):
-            left = jnp.concatenate([keep[p, rows, :] for p in places], axis=0)
-            right = jnp.concatenate([other[p, rows, :] for p in places], axis=0)
+            left = jnp.concatenate([keep_ref[p, rows, :] for p in places], axis=0)
+            right = jnp.concatenate([other_ref[p, rows, :] for p in places], axis=0)
             value = dot(left, grad) + dot(right, other_grad)
             out[...] = value.astype(out.dtype).reshape(len(places), colour.size, width)
 
@@ -360,7 +349,7 @@
     return lax.ppermute(value, "dom", [(i, i ^ 1) for i in range(size)])
 
 
-def product(colours, keep, other, grad, other_grad):
+def product(colours, keep, other, grad, other_grad, spaces):
     width = grad.shape[1]
     outs = []
     for colour in colours:
@@ -369,8 +358,7 @@
         outs.append(((len(kept), colour.size, width), f32))
     ins = (keep, other, grad, other_grad)
     return call(
-        functools.partial(product_kernel, colours), outs, ins, "hhvv", "v" * len(outs),
-        [pltpu.VMEM(keep.shape, bf16)] * 2, 2 * len(colours),
+        functools.partial(product_kernel, colours), outs, ins, "vvvv", spaces * len(colours),
         flops=4 * keep.size * width, moved=keep.size * 12, vmem=16,
     )
 
@@ -429,6 +417,7 @@
     w_two = jnp.swapaxes(w_two, 1, 2)
     self_two = self_two.T
 
+    near = "V" if table <= 2 * rows else "v"
     vm = pltpu.VMEM
     picks_vm, counts_vm = vm((slots, peers), jnp.int32), vm((1, peers), jnp.int32)
     own_vm, total_vm = vm((rows, width), bf16), vm((8, EXTRA), f32)
@@ -451,18 +440,18 @@
     adj, norm, back = call(
         graph_kernel,
         [((all_rows, table), bf16), ((all_rows, EXTRA), f32), ((table, all_rows), bf16)],
-        (edge_src, edge_dst), "hh", "hhh", [edge_vm] * 2 + [adj_vm, norm_vm, back_vm], 5,
+        (edge_src, edge_dst), "hh", near + near + "h", [edge_vm] * 2 + [back_vm], 3,
         flops=4 * all_rows * 256 * table, moved=5 << 20,
     )
     left_one, hidden, packed, total = call(
         first_kernel,
         [((rows, deep), bf16), ((rows, width), bf16), ((boundary, width), bf16), ((8, EXTRA), f32)],
-        (adj, norm, got_one, features, w_one.reshape(deep, width), picks, send_count), "hhhhhhh", "hhhh",
-        [
-            adj_vm, norm_vm, packed_vm, own_vm, vm((deep, width), bf16), picks_vm, counts_vm, left_vm,
+        (adj, norm, got_one, features, w_one.reshape(deep, width), picks, send_count),
+        near + near + "vhhhh", "hhhh",
+        [ own_vm, vm((deep, width), bf16), picks_vm, counts_vm, left_vm,
             own_vm, vm((boundary, width), bf16), total_vm,
         ],
-        7 + relations + 4,
+        10,
         flops=2 * all_rows * width * (table + width), moved=10 << 20,
     )
     got_two = exchange(packed)
@@ -475,27 +464,35 @@
         functools.partial(second_kernel, block),
         [((classes, rows), f32)] + turn_outs
         + [((rows, classes), bf16), ((rows, width), f32), ((boundary, width + EXTRA), bf16)],
-        (me, got_two, adj, norm, back, hidden, w_two, self_two, label_row, total), "shhhhhhhhh", "hhhhhh",
+        (me, got_two, adj, norm, back, hidden, w_two, self_two, label_row, total), "sv" + near + near + "hhhhhh", "hhhhhh",
         [
-            vm((boundary, width), bf16), adj_vm, norm_vm, back_vm, own_vm, vm(w_two.shape, bf16),
+            back_vm, own_vm, vm(w_two.shape, bf16),
             vm(self_two.shape, bf16), vm((1, rows), jnp.int32), total_vm, vm((classes, rows), f32),
             turned_vm, blocks_vm, vm((rows, classes), bf16), vm((all_rows, width), bf16),
             vm((rows, width), f32), packed_vm,
         ],
-        2 + 3 * (relations // 2) + 4 + 6,
+        1 + relations // 2 + 4 + 6,
         flops=8 * all_rows * width * width, moved=16 << 20,
     )
     other_two, other_logits = to_pair(send_two), to_pair(grad_logits)
     returned = exchange(outgoing)
-    parts_two = product(colours, keep_two, other_two, grad_logits, other_logits)
+    keep_two, grad_logits = call(
+        bring_kernel, [turn_outs[0], ((rows, classes), bf16)], (keep_two, grad_logits), "hh", "VV", (), 2,
+        flops=1 << 20, moved=3 << 20, vmem=16,
+    )
+    parts_two = product(colours, keep_two, other_two, grad_logits, other_logits, "Hv")
     grad_pre, loss = call(
         grad_pre_kernel, [((rows, width), bf16), ((1, 1), f32)],
-        (returned, local, parts_two[0], picks, send_count, hidden, total), "vvhhhhh", "vv",
-        [picks_vm, counts_vm, own_vm, total_vm], 4,
-        flops=2 * rows * boundary * width, moved=2 << 20, vmem=50,
+        (returned, parts_two[0], local, hidden, picks, send_count, total), "vhhhhhh", "Vv",
+        [vm((rows, width), f32), own_vm, picks_vm, counts_vm, total_vm], 5,
+        flops=2 * rows * boundary * width, moved=2 << 20,
     )
     other_pre = to_pair(grad_pre)
-    parts_one = product(colours, keep_one, other_one, grad_pre, other_pre)
+    keep_one, other_one = call(
+        bring_kernel, turn_outs, (keep_one, other_one), "hh", "VV", (), 2,
+        flops=1 << 20, moved=5 << 20,
+    )
+    parts_one = product(colours, keep_one, other_one, grad_pre, other_pre, "vv")
     grad_two = scatter_sum(colours, block, parts_two)
     grad_one = scatter_sum(colours, block, parts_one)
     return (logits.T, loss.reshape(()), grad_one, grad_two)

time: 128 us -> 124 us (0.969)
  local copies, waits for them, and re-layouts: 8.49 us -> 4.32 us
  Pallas kernels: 37 us -> 35.1 us
  waiting for transfers between devices: 43 us -> 44.4 us
    all_to_all x3, waiting for transfers between devices: 16 us -> 21 us  [exchange(): got = lax.all_to_all(cut, 'dom', split_axis=0, concat_axis=0, tiled=True)]
    unnamed x19 -> x9, local copies, waits for them, and re-layouts: 8.49 us -> 4.32 us
    ppermute x4, waiting for transfers between devices: 2.35 us -> 0.13 us  [to_pair(): return lax.ppermute(value, 'dom', [(i, i ^ 1) for i in range(size)])]
    pallas_call x28 -> x30, Pallas kernels: 37 us -> 35.1 us  [call(): pl.pallas_call(body, out_shape=[kept[c](s, d) if c in kept else jax.Shape...]
    ppermute x24, waiting for transfers between devices: 24.6 us -> 23.2 us  [across(): return lax.ppermute(value, 'dom', [(i, i ^ 2 << bit) for i in range(size)])]
    ppermute x24, starting transfers between devices: 23.2 us -> 24.6 us  [across(): return lax.ppermute(value, 'dom', [(i, i ^ 2 << bit) for i in range(size)])]
  transfers between devices with their start and end apart: 31 -> 31, of which waited for: 17 -> 15; matrix products, arithmetic and copies ran while one was open for 3% -> 4% of each run, Pallas kernels for 14% -> 15%
where the time goes in v1:
time: 124 us; the launch traced here: 123 us
  waiting for transfers between devices  44.4 us (36%)
  starting transfers between devices  38.1 us (31%)
  Pallas kernels  35.1 us (28%)
  local copies, waits for them, and re-layouts  4.32 us (3%)
    pallas_call x30, Pallas kernels, call(): pl.pallas_call(body, out_shape=[kept[c](s, d) if c in kept else jax.Shape...  35.1 us
    ppermute x24, starting transfers between devices, across(): return lax.ppermute(value, 'dom', [(i, i ^ 2 << bit) for i in range(size)])  24.6 us
    ppermute x24, waiting for transfers between devices, across(): return lax.ppermute(value, 'dom', [(i, i ^ 2 << bit) for i in range(size)])  23.2 us
    all_to_all x3, waiting for transfers between devices, exchange(): got = lax.all_to_all(cut, 'dom', split_axis=0, concat_axis=0, tiled=True)  21 us
    all_to_all x3, starting transfers between devices, exchange(): got = lax.all_to_all(cut, 'dom', split_axis=0, concat_axis=0, tiled=True)  12.7 us
    unnamed x9, local copies, waits for them, and re-layouts  4.32 us
  transfers between devices with their start and end apart: 31, of which 15 were waited for; matrix products, arithmetic and copies ran while one was open for 4% of the time, Pallas kernels for 15%

profile of v1, /device:TPU:0, one launch (start us, length us, event | category | flops | bytes accessed | tf_op | source)
XLA Modules:
  0.0 122.9 jit_solution(3739685511954610612)
XLA Ops:
  0.6 2.2 %shard_map.121 = bf16[256,640]{1,0:T(8,128)(2,1)} custom-call(bf16[256,512]{1,0:T(8,128)(2,1)} %feat_hbm.3, s32[8,32]{1,0:T(8,128)} %bitcast.24, s32[1,32]{1,0:T(1,128)} %count_hbm.5, s32[1,256]{1,0:T(1,128)} %bitcast.27), custom_call_target="tpu_custom_call" | custom-call | flops 67108864 | bytes 600000 | tf_op jit(solution)/shard_map/pallas_call | solution.py:40
  2.8 7.3 %all-to-all-start = ((bf16[32,8,640]{2,1,0:T(8,128)(2,1)}), bf16[32,8,640]{2,1,0:T(8,128)(2,1)S(1)}, u32[]{:S(2)}, u32[]{:S(2)}) async-start(bf16[32,8,640]{2,1,0:T(8,128)(2,1)} %bitcast.4), calls=%async_computation | async-start | bytes 655360 | tf_op jit(solution)/shard_map/all_to_all | solution.py:397
  10.2 5.7 %shard_map.120 = (bf16[2048,512]{1,0:T(8,128)(2,1)S(1)}, f32[2048,128]{1,0:T(8,128)S(1)}, bf16[512,2048]{1,0:T(8,128)(2,1)}) custom-call(s32[8,2,256]{2,1,0:T(2,128)} %src_hbm.1, s32[8,2,256]{2,1,0:T(2,128)} %dst_hbm.1), custom_call_target="tpu_custom_call" | custom-call | flops 1073741824 | bytes 5242880 | tf_op jit(solution)/shard_map/pallas_call | solution.py:40
  15.8 6.4 %all-to-all-done = bf16[32,8,640]{2,1,0:T(8,128)(2,1)S(1)} async-done(((bf16[32,8,640]{2,1,0:T(8,128)(2,1)}), bf16[32,8,640]{2,1,0:T(8,128)(2,1)S(1)}, u32[]{:S(2)}, u32[]{:S(2)}) %all-to-all-start) | async-done | bytes 327712 | tf_op jit(solution)/shard_map/all_to_all | solution.py:397
  22.2 5.1 %shard_map.122 = (bf16[256,4608]{1,0:T(8,128)(2,1)}, bf16[256,512]{1,0:T(8,128)(2,1)}, bf16[256,512]{1,0:T(8,128)(2,1)}, f32[8,128]{1,0:T(8,128)}) custom-call(bf16[2048,512]{1,0:T(8,128)(2,1)S(1)} %get-tuple-element.73.adj, f32[2048,128]{1,0:T(8,128)S(1)} %get-tuple-element.74.norm, bf16[256,640]{1,0:T(8,128)(2,1)S(1)} %bitcast.18, ...), custom_call_target="tpu_custom_call" | custom-call | flops 2147483648 | bytes 10485760 | tf_op jit(solution)/shard_map/pallas_call | solution.py:40
  27.4 2.6 %all-to-all-start.1 = ((bf16[32,8,512]{2,1,0:T(8,128)(2,1)}), bf16[32,8,512]{2,1,0:T(8,128)(2,1)S(1)}, u32[]{:S(2)}, u32[]{:S(2)}) async-start(bf16[32,8,512]{2,1,0:T(8,128)(2,1)} %bitcast.23), calls=%async_computation.1 | async-start | bytes 524288 | tf_op jit(solution)/shard_map/all_to_all | solution.py:397
  30.0 4.3 %copy.15 = bf16[8,512,349]{1,2,0:T(8,128)(2,1)} copy(bf16[8,512,349]{1,0,2:T(8,128)(2,1)} %param.11) | data formatting | bytes 5718016 | tf_op args[2]
  34.3 6.3 %all-to-all-done.1 = bf16[32,8,512]{2,1,0:T(8,128)(2,1)S(1)} async-done(((bf16[32,8,512]{2,1,0:T(8,128)(2,1)}), bf16[32,8,512]{2,1,0:T(8,128)(2,1)S(1)}, u32[]{:S(2)}, u32[]{:S(2)}) %all-to-all-start.1) | async-done | bytes 262176 | tf_op jit(solution)/shard_map/all_to_all | solution.py:397
  40.5 8.6 %shard_map.123 = (f32[349,256]{1,0:T(8,128)}, bf16[16,144,256]{2,1,0:T(8,128)(2,1)}, bf16[16,144,256]{2,1,0:T(8,128)(2,1)}, bf16[256,349]{1,0:T(8,128)(2,1)}, f3...) custom-call(s32[1]{0:T(128)} %bitcast.me_ref, bf16[256,512]{1,0:T(8,128)(2,1)S(1)} %bitcast.20, ...), custom_call_target="tpu_custom_call" | custom-call | flops 4294967296 | bytes 16777216 | tf_op jit(solution)/shard_map/pallas_call | solution.py:40
  49.1 0.1 collective-permute-start
  49.2 3.5 %shard_map.127 = (bf16[16,144,256]{2,1,0:T(8,128)(2,1)}, bf16[16,144,256]{2,1,0:T(8,128)(2,1)}) custom-call(s32[1]{0:T(128)} %bitcast.me_ref, bf16[256,4608]{1,0:T(8,128)(2,1)} %get-tuple-element.89.left_hbm), custom_call_target="tpu_custom_call" | custom-call | flops 1073741824 | bytes 5242880 | tf_op jit(solution)/shard_map/pallas_call | solution.py:40
  52.7 0.6 collective-permute-start.2
  53.3 2.8 %all-to-all-start.2 = ((bf16[32,8,640]{2,1,0:T(8,128)(2,1)}), bf16[32,8,640]{2,1,0:T(8,128)(2,1)S(1)}, u32[]{:S(2)}, u32[]{:S(2)}) async-start(bf16[32,8,640]{2,1,0:T(8,128)(2,1)} %bitcast.12), calls=%async_computation.2 | async-start | bytes 655360 | tf_op jit(solution)/shard_map/all_to_all | solution.py:397
  56.0 0.1 collective-permute-start.1
  56.1 1.3 %shard_map.124 = (bf16[16,144,256]{2,1,0:T(8,128)(2,1)S(1)}, bf16[256,349]{1,0:T(8,128)(2,1)S(1)}) custom-call(bf16[16,144,256]{2,1,0:T(8,128)(2,1)} %get-tuple-element.81.refs_0_, bf16[256,349]{1,0:T(8,128)(2,1)} %get-tuple-element.82.refs_1_), custom_call_target="tpu_custom_call" | custom-call | flops 1048576 | bytes 3145728 | tf_op jit(solution)/shard_map/pallas_call | solution.py:40
  57.4 0.1 collective-permute-done.1.other_grad_ref
  57.6 1.9 %shard_map.125 = (bf16[8,48,349]{2,1,0:T(8,128)(2,1)}, f32[8,48,349]{2,1,0:T(8,128)S(1)}, bf16[8,48,349]{2,1,0:T(8,128)(2,1)}, f32[8,48,349]{2,1,0:T(8,128)S(1)}...) custom-call(bf16[16,144,256]{2,1,0:T(8,128)(2,1)S(1)} %get-tuple-element.83.keep_ref, ...), custom_call_target="tpu_custom_call" | custom-call | flops 823394304 | bytes 7077888 | tf_op jit(solution)/shard_map/pallas_call | solution.py:40
  59.5 8.4 %all-to-all-done.2 = bf16[32,8,640]{2,1,0:T(8,128)(2,1)S(1)} async-done(((bf16[32,8,640]{2,1,0:T(8,128)(2,1)}), bf16[32,8,640]{2,1,0:T(8,128)(2,1)S(1)}, u32[]{:S(2)}, u32[]{:S(2)}) %all-to-all-start.2) | async-done | bytes 327712 | tf_op jit(solution)/shard_map/all_to_all | solution.py:397
  67.9 1.7 %shard_map.126 = (bf16[256,512]{1,0:T(8,128)(2,1)S(1)}, f32[1,1]{1,0:T(1,128)}) custom-call(bf16[256,640]{1,0:T(8,128)(2,1)S(1)} %bitcast.19, bf16[8,48,349]{2,1,0:T(8,128)(2,1)} %get-tuple-element.86.after_ref, f32[256,512]{1,0:T(8,128)} %get-tuple-element.87.local_hbm, bf16[256,512]{1,0:T(8,128)(2,1)} %get-tuple-element.77.hid_hbm, s32[8,32]{1,0:T(8,128)} %bitcast.26, ...), custom_call_target="tpu_custom_call" | custom-call | flops 67108864 | bytes 2097152 | tf_op jit(solution)/shard_map/pallas_call | solution.py:40
  69.6 0.1 collective-permute-start.3
  69.7 1.7 %shard_map.128 = (bf16[16,144,256]{2,1,0:T(8,128)(2,1)S(1)}, bf16[16,144,256]{2,1,0:T(8,128)(2,1)S(1)}) custom-call(bf16[16,144,256]{2,1,0:T(8,128)(2,1)} %get-tuple-element.90.refs_0_, bf16[16,144,256]{2,1,0:T(8,128)(2,1)} %collective-permute-done.2.refs_1_), custom_call_target="tpu_custom_call" | custom-call | flops 1048576 | bytes 5242880 | tf_op jit(solution)/shard_map/pallas_call | solution.py:40
  71.4 0.8 collective-permute-start.20
  72.2 1.4 %shard_map.129 = (bf16[8,48,512]{2,1,0:T(8,128)(2,1)S(1)}, f32[8,48,512]{2,1,0:T(8,128)S(1)}, bf16[8,48,512]{2,1,0:T(8,128)(2,1)S(1)}, f32[8,48,512]{2,1,0:T(8,1...) custom-call(bf16[16,144,256]{2,1,0:T(8,128)(2,1)S(1)} %get-tuple-element.92.keep_ref, ...), custom_call_target="tpu_custom_call" | custom-call | flops 1207959552 | bytes 7077888 | tf_op jit(solution)/shard_map/pallas_call | solution.py:40
  73.6 1.0 collective-permute-start.4
  74.6 1.0 collective-permute-start.8
  75.6 0.7 collective-permute-start.12
  76.3 1.4 %collective-permute-start.24 = (bf16[8,48,349]{2,1,0:T(8,128)(2,1)S(1)}, bf16[8,48,349]{2,1,0:T(8,128)(2,1)S(1)}, u32[]{:S(2)}, u32[]{:S(2)}) collective-permute-start(bf16[8,48,349]{2,1,0:T(8,128)(2,1)S(1)} %copy-done.2), channel_id=1, source_target_pairs={{0,8},{1,9},{2,10},{3,11},{4,12},{5,13},{6,14},{7,15},{8,0},{9,1},... | collective-permute-start | bytes 804104 | tf_op jit(solution)/shard_map/ppermute | solution.py:344
  77.7 3.7 %collective-permute-done.20.got = bf16[8,48,349]{2,1,0:T(8,128)(2,1)S(1)} collective-permute-done((bf16[8,48,349]{2,1,0:T(8,128)(2,1)S(1)}, bf16[8,48,349]{2,1,0:T(8,128)(2,1)S(1)}, u32[]{:S(2)}, u32[]{:S(2)}) %collective-permute-start.20) | collective-permute-done | bytes 268064 | tf_op jit(solution)/shard_map/ppermute | solution.py:344
  81.4 0.7 collective-permute-start.16
  82.0 0.1 shard_map.143
  82.1 3.6 %collective-permute-done.4.got = bf16[8,48,512]{2,1,0:T(8,128)(2,1)S(1)} collective-permute-done((bf16[8,48,512]{2,1,0:T(8,128)(2,1)S(1)}, bf16[8,48,512]{2,1,0:T(8,128)(2,1)S(1)}, u32[]{:S(2)}, u32[]{:S(2)}) %collective-permute-start.4) | collective-permute-done | bytes 393248 | tf_op jit(solution)/shard_map/ppermute | solution.py:344
  85.7 0.9 collective-permute-start.21
  86.6 0.1 shard_map.130
  86.7 2.6 %collective-permute-done.8.got = bf16[8,48,512]{2,1,0:T(8,128)(2,1)S(1)} collective-permute-done((bf16[8,48,512]{2,1,0:T(8,128)(2,1)S(1)}, bf16[8,48,512]{2,1,0:T(8,128)(2,1)S(1)}, u32[]{:S(2)}, u32[]{:S(2)}) %collective-permute-start.8) | collective-permute-done | bytes 393248 | tf_op jit(solution)/shard_map/ppermute | solution.py:344
  89.3 0.8 collective-permute-start.5
  90.1 0.1 shard_map.133
  90.2 0.2 collective-permute-start.9
  90.3 0.1 shard_map.136
  90.4 2.7 %collective-permute-done.24.got = bf16[8,48,349]{2,1,0:T(8,128)(2,1)S(1)} collective-permute-done((bf16[8,48,349]{2,1,0:T(8,128)(2,1)S(1)}, bf16[8,48,349]{2,1,0:T(8,128)(2,1)S(1)}, u32[]{:S(2)}, u32[]{:S(2)}) %collective-permute-start.24) | collective-permute-done | bytes 268064 | tf_op jit(solution)/shard_map/ppermute | solution.py:344
  93.1 1.9 %collective-permute-start.13 = (bf16[4,48,512]{2,1,0:T(8,128)(2,1)S(1)}, bf16[4,48,512]{2,1,0:T(8,128)(2,1)S(1)}, u32[]{:S(2)}, u32[]{:S(2)}) collective-permute-start(bf16[4,48,512]{2,1,0:T(8,128)(2,1)S(1)} %get-tuple-element.113), channel_id=1, source_target_pairs={{0,4},{1,5},{2,6},{3,7},{4,0},{5,1},{6,2},{7,3},{8,12},{9,13},{10,... | collective-permute-start | bytes 589832 | tf_op jit(solution)/shard_map/ppermute | solution.py:344
  95.0 0.1 shard_map.146
  95.0 0.2 collective-permute-start.25
  95.2 0.1 shard_map.140
  95.3 0.8 collective-permute-start.17
  96.2 0.5 collective-permute-done.5.got
  96.7 0.9 collective-permute-start.22
  97.6 1.0 collective-permute-done.9.got
  98.6 1.3 %collective-permute-start.6 = (bf16[2,48,512]{2,1,0:T(8,128)(2,1)S(1)}, bf16[2,48,512]{2,1,0:T(8,128)(2,1)S(1)}, u32[]{:S(2)}, u32[]{:S(2)}) collective-permute-start(bf16[2,48,512]{2,1,0:T(8,128)(2,1)S(1)} %get-tuple-element.99), channel_id=1, source_target_pairs={{0,4},{1,5},{2,6},{3,7},{4,0},{5,1},{6,2},{7,3},{8,12},{9,13},{10,... | collective-permute-start | bytes 294920 | tf_op jit(solution)/shard_map/ppermute | solution.py:344
  99.9 0.8 collective-permute-start.10
  100.8 0.1 collective-permute-done.25.got
  100.9 1.9 %collective-permute-start.14 = (bf16[2,48,512]{2,1,0:T(8,128)(2,1)S(1)}, bf16[2,48,512]{2,1,0:T(8,128)(2,1)S(1)}, u32[]{:S(2)}, u32[]{:S(2)}) collective-permute-start(bf16[2,48,512]{2,1,0:T(8,128)(2,1)S(1)} %get-tuple-element.115), channel_id=1, source_target_pairs={{0,16},{1,17},{2,18},{3,19},{4,20},{5,21},{6,22},{7,23},{8,24},{9,... | collective-permute-start | bytes 294920 | tf_op jit(solution)/shard_map/ppermute | solution.py:344
  102.9 1.1 collective-permute-start.26
  104.0 2.1 %collective-permute-start.18 = (bf16[2,48,349]{2,1,0:T(8,128)(2,1)S(1)}, bf16[2,48,349]{2,1,0:T(8,128)(2,1)S(1)}, u32[]{:S(2)}, u32[]{:S(2)}) collective-permute-start(bf16[2,48,349]{2,1,0:T(8,128)(2,1)S(1)} %get-tuple-element.122), channel_id=1, source_target_pairs={{0,4},{1,5},{2,6},{3,7},{4,0},{5,1},{6,2},{7,3},{8,12},{9,13},{10,... | collective-permute-start | bytes 201032 | tf_op jit(solution)/shard_map/ppermute | solution.py:344
  106.1 0.7 collective-permute-start.23
  106.8 2.3 %collective-permute-start.7 = (bf16[1,48,512]{2,1,0:T(8,128)(2,1)S(1)}, bf16[1,48,512]{2,1,0:T(8,128)(2,1)S(1)}, u32[]{:S(2)}, u32[]{:S(2)}) collective-permute-start(bf16[1,48,512]{2,1,0:T(8,128)(2,1)S(1)} %get-tuple-element.101), channel_id=1, source_target_pairs={{0,16},{1,17},{2,18},{3,19},{4,20},{5,21},{6,22},{7,23},{8,24},{9,... | collective-permute-start | bytes 147464 | tf_op jit(solution)/shard_map/ppermute | solution.py:344
  109.2 3.1 %collective-permute-done.14.got = bf16[2,48,512]{2,1,0:T(8,128)(2,1)S(1)} collective-permute-done((bf16[2,48,512]{2,1,0:T(8,128)(2,1)S(1)}, bf16[2,48,512]{2,1,0:T(8,128)(2,1)S(1)}, u32[]{:S(2)}, u32[]{:S(2)}) %collective-permute-start.14) | collective-permute-done | bytes 98336 | tf_op jit(solution)/shard_map/ppermute | solution.py:344
  112.3 2.1 %collective-permute-done.26.got = bf16[2,48,349]{2,1,0:T(8,128)(2,1)S(1)} collective-permute-done((bf16[2,48,349]{2,1,0:T(8,128)(2,1)S(1)}, bf16[2,48,349]{2,1,0:T(8,128)(2,1)S(1)}, u32[]{:S(2)}, u32[]{:S(2)}) %collective-permute-start.26) | collective-permute-done | bytes 67040 | tf_op jit(solution)/shard_map/ppermute | solution.py:344
  114.4 1.1 collective-permute-start.15
  115.4 1.0 collective-permute-start.27
  116.5 1.0 collective-permute-start.19
  117.5 2.0 %collective-permute-done.27.refs_4_ = bf16[1,48,349]{2,1,0:T(8,128)(2,1)S(1)} collective-permute-done((bf16[1,48,349]{2,1,0:T(8,128)(2,1)S(1)}, bf16[1,48,349]{2,1,0:T(8,128)(2,1)S(1)}, u32[]{:S(2)}, u32[]{:S(2)}) %collective-permute-start.27) | collective-permute-done | bytes 33536 | tf_op jit(solution)/shard_map/ppermute | solution.py:344
  119.5 2.0 %collective-permute-done.19.refs_0_ = bf16[1,48,349]{2,1,0:T(8,128)(2,1)S(1)} collective-permute-done((bf16[1,48,349]{2,1,0:T(8,128)(2,1)S(1)}, bf16[1,48,349]{2,1,0:T(8,128)(2,1)S(1)}, u32[]{:S(2)}, u32[]{:S(2)}) %collective-permute-start.19) | collective-permute-done | bytes 33536 | tf_op jit(solution)/shard_map/ppermute | solution.py:344
  121.4 0.7 shard_map.149
  122.1 0.7 shard_map.139
  (37 shorter events, 0.3 us)
Async XLA Ops:
  2.8 19.4 %all-to-all-start = ((bf16[32,8,640]{2,1,0:T(8,128)(2,1)}), bf16[32,8,640]{2,1,0:T(8,128)(2,1)S(1)}, u32[]{:S(2)}, u32[]{:S(2)}) async-start(bf16[32,8,640]{2,1,0:T(8,128)(2,1)} %bitcast.4), calls=%async_computation | async-start | bytes 655360 | tf_op jit(solution)/shard_map/all_to_all | solution.py:397
  27.4 13.2 %all-to-all-start.1 = ((bf16[32,8,512]{2,1,0:T(8,128)(2,1)}), bf16[32,8,512]{2,1,0:T(8,128)(2,1)S(1)}, u32[]{:S(2)}, u32[]{:S(2)}) async-start(bf16[32,8,512]{2,1,0:T(8,128)(2,1)} %bitcast.23), calls=%async_computation.1 | async-start | bytes 524288 | tf_op jit(solution)/shard_map/all_to_all | solution.py:397
  49.1 8.4 %collective-permute-start = (bf16[16,144,256]{2,1,0:T(8,128)(2,1)}, bf16[16,144,256]{2,1,0:T(8,128)(2,1)S(1)}, u32[]{:S(2)}, u32[]{:S(2)}) collective-permute-start(bf16[16,144,256]{2,1,0:T(8,128)(2,1)} %get-tuple-element.84), channel_id=1, source_target_pairs={{0,1},{1,0},{2,3},{3,2},{4,5},{5,4},{6,7},{7,6},{8,9},{9,8},{10,11... | collective-permute-start | bytes 3538952 | tf_op jit(solution)/shard_map/ppermute | solution.py:349
  49.2 6.8 %copy-start.1 = (bf16[256,349]{1,0:T(8,128)(2,1)S(1)}, bf16[256,349]{1,0:T(8,128)(2,1)}, u32[]{:S(2)}) copy-start(bf16[256,349]{1,0:T(8,128)(2,1)} %get-tuple-element.82.refs_1_) | copy-start | bytes 536068
  52.7 17.0 %collective-permute-start.2 = (bf16[16,144,256]{2,1,0:T(8,128)(2,1)}, bf16[16,144,256]{2,1,0:T(8,128)(2,1)}, u32[]{:S(2)}, u32[]{:S(2)}) collective-permute-start(bf16[16,144,256]{2,1,0:T(8,128)(2,1)} %get-tuple-element.91), channel_id=1, source_target_pairs={{0,1},{1,0},{2,3},{3,2},{4,5},{5,4},{6,7},{7,6},{8,9},{9,8},{10,11... | collective-permute-start | bytes 3538952 | tf_op jit(solution)/shard_map/ppermute | solution.py:349
  53.3 14.6 %all-to-all-start.2 = ((bf16[32,8,640]{2,1,0:T(8,128)(2,1)}), bf16[32,8,640]{2,1,0:T(8,128)(2,1)S(1)}, u32[]{:S(2)}, u32[]{:S(2)}) async-start(bf16[32,8,640]{2,1,0:T(8,128)(2,1)} %bitcast.12), calls=%async_computation.2 | async-start | bytes 655360 | tf_op jit(solution)/shard_map/all_to_all | solution.py:397
  56.0 1.5 %collective-permute-start.1 = (bf16[256,349]{1,0:T(8,128)(2,1)S(1)}, bf16[256,349]{1,0:T(8,128)(2,1)S(1)}, u32[]{:S(2)}, u32[]{:S(2)}) collective-permute-start(bf16[256,349]{1,0:T(8,128)(2,1)S(1)} %copy-done.1), channel_id=1, source_target_pairs={{0,1},{1,0},{2,3},{3,2},{4,5},{5,4},{6,7},{7,6},{8,9},{9,8},{10,11... | collective-permute-start | bytes 536072 | tf_op jit(solution)/shard_map/ppermute | solution.py:349
  69.6 2.6 %collective-permute-start.3 = (bf16[256,512]{1,0:T(8,128)(2,1)S(1)}, bf16[256,512]{1,0:T(8,128)(2,1)S(1)}, u32[]{:S(2)}, u32[]{:S(2)}) collective-permute-start(bf16[256,512]{1,0:T(8,128)(2,1)S(1)} %get-tuple-element.94.grad_ref), channel_id=1, source_target_pairs={{0,1},{1,0},{2,3},{3,2},{4,5},{5,4},{6,7},{7,6},{8,9},{9,8},{10,11... | collective-permute-start | bytes 786440 | tf_op jit(solution)/shard_map/ppermute | solution.py:349
  69.7 1.7 %copy-start.3 = (bf16[8,48,349]{2,1,0:T(8,128)(2,1)S(1)}, bf16[8,48,349]{2,1,0:T(8,128)(2,1)}, u32[]{:S(2)}) copy-start(bf16[8,48,349]{2,1,0:T(8,128)(2,1)} %get-tuple-element.126) | copy-start | bytes 804100
  71.4 9.9 %collective-permute-start.20 = (bf16[8,48,349]{2,1,0:T(8,128)(2,1)S(1)}, bf16[8,48,349]{2,1,0:T(8,128)(2,1)S(1)}, u32[]{:S(2)}, u32[]{:S(2)}) collective-permute-start(bf16[8,48,349]{2,1,0:T(8,128)(2,1)S(1)} %copy-done.3), channel_id=1, source_target_pairs={{0,4},{1,5},{2,6},{3,7},{4,0},{5,1},{6,2},{7,3},{8,12},{9,13},{10,... | collective-permute-start | bytes 804104 | tf_op jit(solution)/shard_map/ppermute | solution.py:344
  72.2 4.1 %copy-start.2 = (bf16[8,48,349]{2,1,0:T(8,128)(2,1)S(1)}, bf16[8,48,349]{2,1,0:T(8,128)(2,1)}, u32[]{:S(2)}) copy-start(bf16[8,48,349]{2,1,0:T(8,128)(2,1)} %get-tuple-element.134) | copy-start | bytes 804100
  72.2 9.1 %copy-start = (bf16[8,48,349]{2,1,0:T(8,128)(2,1)S(1)}, bf16[8,48,349]{2,1,0:T(8,128)(2,1)}, u32[]{:S(2)}) copy-start(bf16[8,48,349]{2,1,0:T(8,128)(2,1)} %get-tuple-element.86.after_ref) | copy-start | bytes 804100
  73.6 12.1 %collective-permute-start.4 = (bf16[8,48,512]{2,1,0:T(8,128)(2,1)S(1)}, bf16[8,48,512]{2,1,0:T(8,128)(2,1)S(1)}, u32[]{:S(2)}, u32[]{:S(2)}) collective-permute-start(bf16[8,48,512]{2,1,0:T(8,128)(2,1)S(1)} %get-tuple-element.95), channel_id=1, source_target_pairs={{0,2},{1,3},{2,0},{3,1},{4,6},{5,7},{6,4},{7,5},{8,10},{9,11},{10,... | collective-permute-start | bytes 1179656 | tf_op jit(solution)/shard_map/ppermute | solution.py:344
  74.6 14.7 %collective-permute-start.8 = (bf16[8,48,512]{2,1,0:T(8,128)(2,1)S(1)}, bf16[8,48,512]{2,1,0:T(8,128)(2,1)S(1)}, u32[]{:S(2)}, u32[]{:S(2)}) collective-permute-start(bf16[8,48,512]{2,1,0:T(8,128)(2,1)S(1)} %get-tuple-element.103), channel_id=1, source_target_pairs={{0,4},{1,5},{2,6},{3,7},{4,0},{5,1},{6,2},{7,3},{8,12},{9,13},{10,... | collective-permute-start | bytes 1179656 | tf_op jit(solution)/shard_map/ppermute | solution.py:344
  75.6 14.5 %collective-permute-start.12 = (bf16[8,48,512]{2,1,0:T(8,128)(2,1)S(1)}, bf16[8,48,512]{2,1,0:T(8,128)(2,1)S(1)}, u32[]{:S(2)}, u32[]{:S(2)}) collective-permute-start(bf16[8,48,512]{2,1,0:T(8,128)(2,1)S(1)} %get-tuple-element.111), channel_id=1, source_target_pairs={{0,8},{1,9},{2,10},{3,11},{4,12},{5,13},{6,14},{7,15},{8,0},{9,1},... | collective-permute-start | bytes 1179656 | tf_op jit(solution)/shard_map/ppermute | solution.py:344
  76.3 16.8 %collective-permute-start.24 = (bf16[8,48,349]{2,1,0:T(8,128)(2,1)S(1)}, bf16[8,48,349]{2,1,0:T(8,128)(2,1)S(1)}, u32[]{:S(2)}, u32[]{:S(2)}) collective-permute-start(bf16[8,48,349]{2,1,0:T(8,128)(2,1)S(1)} %copy-done.2), channel_id=1, source_target_pairs={{0,8},{1,9},{2,10},{3,11},{4,12},{5,13},{6,14},{7,15},{8,0},{9,1},... | collective-permute-start | bytes 804104 | tf_op jit(solution)/shard_map/ppermute | solution.py:344
  81.4 13.6 %collective-permute-start.16 = (bf16[8,48,349]{2,1,0:T(8,128)(2,1)S(1)}, bf16[8,48,349]{2,1,0:T(8,128)(2,1)S(1)}, u32[]{:S(2)}, u32[]{:S(2)}) collective-permute-start(bf16[8,48,349]{2,1,0:T(8,128)(2,1)S(1)} %copy-done), channel_id=1, source_target_pairs={{0,2},{1,3},{2,0},{3,1},{4,6},{5,7},{6,4},{7,5},{8,10},{9,11},{10,... | collective-permute-start | bytes 804104 | tf_op jit(solution)/shard_map/ppermute | solution.py:344
  85.7 9.6 %collective-permute-start.21 = (bf16[4,48,349]{2,1,0:T(8,128)(2,1)S(1)}, bf16[4,48,349]{2,1,0:T(8,128)(2,1)S(1)}, u32[]{:S(2)}, u32[]{:S(2)}) collective-permute-start(bf16[4,48,349]{2,1,0:T(8,128)(2,1)S(1)} %get-tuple-element.128), channel_id=1, source_target_pairs={{0,2},{1,3},{2,0},{3,1},{4,6},{5,7},{6,4},{7,5},{8,10},{9,11},{10,... | collective-permute-start | bytes 402056 | tf_op jit(solution)/shard_map/ppermute | solution.py:344
  89.3 7.4 %collective-permute-start.5 = (bf16[4,48,512]{2,1,0:T(8,128)(2,1)S(1)}, bf16[4,48,512]{2,1,0:T(8,128)(2,1)S(1)}, u32[]{:S(2)}, u32[]{:S(2)}) collective-permute-start(bf16[4,48,512]{2,1,0:T(8,128)(2,1)S(1)} %get-tuple-element.97), channel_id=1, source_target_pairs={{0,8},{1,9},{2,10},{3,11},{4,12},{5,13},{6,14},{7,15},{8,0},{9,1},... | collective-permute-start | bytes 589832 | tf_op jit(solution)/shard_map/ppermute | solution.py:344
  90.2 8.4 %collective-permute-start.9 = (bf16[4,48,512]{2,1,0:T(8,128)(2,1)S(1)}, bf16[4,48,512]{2,1,0:T(8,128)(2,1)S(1)}, u32[]{:S(2)}, u32[]{:S(2)}) collective-permute-start(bf16[4,48,512]{2,1,0:T(8,128)(2,1)S(1)} %get-tuple-element.105), channel_id=1, source_target_pairs={{0,2},{1,3},{2,0},{3,1},{4,6},{5,7},{6,4},{7,5},{8,10},{9,11},{10,... | collective-permute-start | bytes 589832 | tf_op jit(solution)/shard_map/ppermute | solution.py:344
  93.1 6.8 %collective-permute-start.13 = (bf16[4,48,512]{2,1,0:T(8,128)(2,1)S(1)}, bf16[4,48,512]{2,1,0:T(8,128)(2,1)S(1)}, u32[]{:S(2)}, u32[]{:S(2)}) collective-permute-start(bf16[4,48,512]{2,1,0:T(8,128)(2,1)S(1)} %get-tuple-element.113), channel_id=1, source_target_pairs={{0,4},{1,5},{2,6},{3,7},{4,0},{5,1},{6,2},{7,3},{8,12},{9,13},{10,... | collective-permute-start | bytes 589832 | tf_op jit(solution)/shard_map/ppermute | solution.py:344
  95.0 5.9 %collective-permute-start.25 = (bf16[4,48,349]{2,1,0:T(8,128)(2,1)S(1)}, bf16[4,48,349]{2,1,0:T(8,128)(2,1)S(1)}, u32[]{:S(2)}, u32[]{:S(2)}) collective-permute-start(bf16[4,48,349]{2,1,0:T(8,128)(2,1)S(1)} %get-tuple-element.136), channel_id=1, source_target_pairs={{0,4},{1,5},{2,6},{3,7},{4,0},{5,1},{6,2},{7,3},{8,12},{9,13},{10,... | collective-permute-start | bytes 402056 | tf_op jit(solution)/shard_map/ppermute | solution.py:344
  95.3 7.6 %collective-permute-start.17 = (bf16[4,48,349]{2,1,0:T(8,128)(2,1)S(1)}, bf16[4,48,349]{2,1,0:T(8,128)(2,1)S(1)}, u32[]{:S(2)}, u32[]{:S(2)}) collective-permute-start(bf16[4,48,349]{2,1,0:T(8,128)(2,1)S(1)} %get-tuple-element.120), channel_id=1, source_target_pairs={{0,8},{1,9},{2,10},{3,11},{4,12},{5,13},{6,14},{7,15},{8,0},{9,1},... | collective-permute-start | bytes 402056 | tf_op jit(solution)/shard_map/ppermute | solution.py:344
  96.7 7.3 %collective-permute-start.22 = (bf16[2,48,349]{2,1,0:T(8,128)(2,1)S(1)}, bf16[2,48,349]{2,1,0:T(8,128)(2,1)S(1)}, u32[]{:S(2)}, u32[]{:S(2)}) collective-permute-start(bf16[2,48,349]{2,1,0:T(8,128)(2,1)S(1)} %get-tuple-element.130), channel_id=1, source_target_pairs={{0,8},{1,9},{2,10},{3,11},{4,12},{5,13},{6,14},{7,15},{8,0},{9,1},... | collective-permute-start | bytes 201032 | tf_op jit(solution)/shard_map/ppermute | solution.py:344
  98.6 7.5 %collective-permute-start.6 = (bf16[2,48,512]{2,1,0:T(8,128)(2,1)S(1)}, bf16[2,48,512]{2,1,0:T(8,128)(2,1)S(1)}, u32[]{:S(2)}, u32[]{:S(2)}) collective-permute-start(bf16[2,48,512]{2,1,0:T(8,128)(2,1)S(1)} %get-tuple-element.99), channel_id=1, source_target_pairs={{0,4},{1,5},{2,6},{3,7},{4,0},{5,1},{6,2},{7,3},{8,12},{9,13},{10,... | collective-permute-start | bytes 294920 | tf_op jit(solution)/shard_map/ppermute | solution.py:344
  99.9 6.9 %collective-permute-start.10 = (bf16[2,48,512]{2,1,0:T(8,128)(2,1)S(1)}, bf16[2,48,512]{2,1,0:T(8,128)(2,1)S(1)}, u32[]{:S(2)}, u32[]{:S(2)}) collective-permute-start(bf16[2,48,512]{2,1,0:T(8,128)(2,1)S(1)} %get-tuple-element.107), channel_id=1, source_target_pairs={{0,8},{1,9},{2,10},{3,11},{4,12},{5,13},{6,14},{7,15},{8,0},{9,1},... | collective-permute-start | bytes 294920 | tf_op jit(solution)/shard_map/ppermute | solution.py:344
  100.9 11.4 %collective-permute-start.14 = (bf16[2,48,512]{2,1,0:T(8,128)(2,1)S(1)}, bf16[2,48,512]{2,1,0:T(8,128)(2,1)S(1)}, u32[]{:S(2)}, u32[]{:S(2)}) collective-permute-start(bf16[2,48,512]{2,1,0:T(8,128)(2,1)S(1)} %get-tuple-element.115), channel_id=1, source_target_pairs={{0,16},{1,17},{2,18},{3,19},{4,20},{5,21},{6,22},{7,23},{8,24},{9,... | collective-permute-start | bytes 294920 | tf_op jit(solution)/shard_map/ppermute | solution.py:344
  102.9 11.5 %collective-permute-start.26 = (bf16[2,48,349]{2,1,0:T(8,128)(2,1)S(1)}, bf16[2,48,349]{2,1,0:T(8,128)(2,1)S(1)}, u32[]{:S(2)}, u32[]{:S(2)}) collective-permute-start(bf16[2,48,349]{2,1,0:T(8,128)(2,1)S(1)} %get-tuple-element.138), channel_id=1, source_target_pairs={{0,16},{1,17},{2,18},{3,19},{4,20},{5,21},{6,22},{7,23},{8,24},{9,... | collective-permute-start | bytes 201032 | tf_op jit(solution)/shard_map/ppermute | solution.py:344
  104.0 11.5 %collective-permute-start.18 = (bf16[2,48,349]{2,1,0:T(8,128)(2,1)S(1)}, bf16[2,48,349]{2,1,0:T(8,128)(2,1)S(1)}, u32[]{:S(2)}, u32[]{:S(2)}) collective-permute-start(bf16[2,48,349]{2,1,0:T(8,128)(2,1)S(1)} %get-tuple-element.122), channel_id=1, source_target_pairs={{0,4},{1,5},{2,6},{3,7},{4,0},{5,1},{6,2},{7,3},{8,12},{9,13},{10,... | collective-permute-start | bytes 201032 | tf_op jit(solution)/shard_map/ppermute | solution.py:344
  106.1 10.4 %collective-permute-start.23 = (bf16[1,48,349]{2,1,0:T(8,128)(2,1)S(1)}, bf16[1,48,349]{2,1,0:T(8,128)(2,1)S(1)}, u32[]{:S(2)}, u32[]{:S(2)}) collective-permute-start(bf16[1,48,349]{2,1,0:T(8,128)(2,1)S(1)} %get-tuple-element.132), channel_id=1, source_target_pairs={{0,16},{1,17},{2,18},{3,19},{4,20},{5,21},{6,22},{7,23},{8,24},{9,... | collective-permute-start | bytes 100520 | tf_op jit(solution)/shard_map/ppermute | solution.py:344
  106.8 15.3 %collective-permute-start.7 = (bf16[1,48,512]{2,1,0:T(8,128)(2,1)S(1)}, bf16[1,48,512]{2,1,0:T(8,128)(2,1)S(1)}, u32[]{:S(2)}, u32[]{:S(2)}) collective-permute-start(bf16[1,48,512]{2,1,0:T(8,128)(2,1)S(1)} %get-tuple-element.101), channel_id=1, source_target_pairs={{0,16},{1,17},{2,18},{3,19},{4,20},{5,21},{6,22},{7,23},{8,24},{9,... | collective-permute-start | bytes 147464 | tf_op jit(solution)/shard_map/ppermute | solution.py:344
  112.3 9.9 %collective-permute-start.11 = (bf16[1,48,512]{2,1,0:T(8,128)(2,1)S(1)}, bf16[1,48,512]{2,1,0:T(8,128)(2,1)S(1)}, u32[]{:S(2)}, u32[]{:S(2)}) collective-permute-start(bf16[1,48,512]{2,1,0:T(8,128)(2,1)S(1)} %get-tuple-element.109), channel_id=1, source_target_pairs={{0,16},{1,17},{2,18},{3,19},{4,20},{5,21},{6,22},{7,23},{8,24},{9,... | collective-permute-start | bytes 147464 | tf_op jit(solution)/shard_map/ppermute | solution.py:344
  114.4 7.8 %collective-permute-start.15 = (bf16[1,48,512]{2,1,0:T(8,128)(2,1)S(1)}, bf16[1,48,512]{2,1,0:T(8,128)(2,1)S(1)}, u32[]{:S(2)}, u32[]{:S(2)}) collective-permute-start(bf16[1,48,512]{2,1,0:T(8,128)(2,1)S(1)} %get-tuple-element.117), channel_id=1, source_target_pairs={{0,2},{1,3},{2,0},{3,1},{4,6},{5,7},{6,4},{7,5},{8,10},{9,11},{10,... | collective-permute-start | bytes 147464 | tf_op jit(solution)/shard_map/ppermute | solution.py:344
  115.4 4.0 %collective-permute-start.27 = (bf16[1,48,349]{2,1,0:T(8,128)(2,1)S(1)}, bf16[1,48,349]{2,1,0:T(8,128)(2,1)S(1)}, u32[]{:S(2)}, u32[]{:S(2)}) collective-permute-start(bf16[1,48,349]{2,1,0:T(8,128)(2,1)S(1)} %get-tuple-element.140), channel_id=1, source_target_pairs={{0,2},{1,3},{2,0},{3,1},{4,6},{5,7},{6,4},{7,5},{8,10},{9,11},{10,... | collective-permute-start | bytes 100520 | tf_op jit(solution)/shard_map/ppermute | solution.py:344
  116.5 4.9 %collective-permute-start.19 = (bf16[1,48,349]{2,1,0:T(8,128)(2,1)S(1)}, bf16[1,48,349]{2,1,0:T(8,128)(2,1)S(1)}, u32[]{:S(2)}, u32[]{:S(2)}) collective-permute-start(bf16[1,48,349]{2,1,0:T(8,128)(2,1)S(1)} %get-tuple-element.124), channel_id=1, source_target_pairs={{0,16},{1,17},{2,18},{3,19},{4,20},{5,21},{6,22},{7,23},{8,24},{9,... | collective-permute-start | bytes 100520 | tf_op jit(solution)/shard_map/ppermute | solution.py:344

commit v2 on v1

--- a/solution.py
+++ b/solution.py
@@ -69,7 +69,10 @@
     chosen = jnp.where(iota((slots, peers), 0) < counts, picks, -1).astype(f32)
     lane = iota((peers, peers * slots), 1)
     spreader = jnp.where(iota((peers, peers * slots), 0) == lane // slots, 1.0, 0.0)
-    laid = jnp.dot(chosen, spreader, preferred_element_type=f32, precision=lax.Precision.HIGHEST)
+    if rows <= 256:
+        laid = dot(chosen.astype(bf16), spreader.astype(bf16))
+    else:
+        laid = jnp.dot(chosen, spreader, preferred_element_type=f32, precision=lax.Precision.HIGHEST)
     mine = iota((slots, peers * slots), 0) == iota((slots, peers * slots), 1) % slots
     row = jnp.sum(jnp.where(mine, laid, 0.0), axis=0, keepdims=True)
     hot = iota((rows, peers * slots), 0) == jnp.round(row).astype(jnp.int32)
@@ -79,20 +82,22 @@
 def pack_kernel(feat_hbm, picks_hbm, count_hbm, label_hbm, out_ref, feat, picks, counts, label, sems):
     copies = Copies(sems)
     pairs = ((picks_hbm, picks), (count_hbm, counts), (label_hbm, label), (feat_hbm, feat))
-    wait_all([copies.start(a, b) for a, b in pairs])
+    ins = [copies.start(a, b) for a, b in pairs]
     rows, width = feat.shape
     slots = out_ref.shape[0]
+    wait_all(ins[:3])
     hot = pick_hot(picks[...], counts[...], rows)
-    out_ref[:, :width] = dot_tn(hot, feat[...]).astype(bf16)
     count = jnp.sum(jnp.where(label[...] >= 0, 1.0, 0.0), axis=1, keepdims=True)
     high = jnp.floor(count * (1.0 / 128.0))
     low = count - 128.0 * high
     lane = iota((slots, EXTRA), 1)
     out_ref[:, width:] = jnp.where(lane < 64, high, low).astype(bf16)
+    ins[3].wait()
+    out_ref[:, :width] = dot_tn(hot, feat[...]).astype(bf16)
 
 
 def graph_kernel(
-    src_hbm, dst_hbm, adj_ref, norm_ref, back_hbm, src_ref, dst_ref, back_ref, sems
+    src_hbm, dst_hbm, adj_ref, count_ref, back_hbm, src_ref, dst_ref, back_ref, sems
 ):
     copies = Copies(sems)
     wait_all([copies.start(src_hbm, src_ref), copies.start(dst_hbm, dst_ref)])
@@ -110,15 +115,15 @@
             hot_dst = hot_dst.astype(bf16)
             adj_ref[pl.ds(start, 128), :] = dot_nt(hot_dst, hot_src).astype(bf16)
             back_ref[:, pl.ds(start, 128)] = dot_nt(hot_src, hot_dst).astype(bf16)
-            norm = 1.0 / jnp.maximum(count, 1.0)
-            norm_ref[pl.ds(start, 128), :] = jnp.broadcast_to(norm, (128, EXTRA))
+            count_ref[pl.ds(start, 128), :] = jnp.broadcast_to(count, (128, EXTRA)).astype(bf16)
         return carry
 
     lax.fori_loop(0, relations, step, 0)
     copies.start(back_ref, back_hbm).wait()
 
 
-def wide(norm, width):
+def norm_of(counts, width):
+    norm = 1.0 / jnp.maximum(counts.astype(f32), 1.0)
     return jnp.concatenate([norm] * (width // EXTRA), axis=1)
 
 
@@ -135,8 +140,8 @@
 
 def first_kernel(
     adj, norm, got_ref, feat_hbm, w_hbm, picks_hbm, count_hbm,
-    left_hbm, hid_hbm, pack_hbm, total_hbm,
-    feat, w, picks, counts, left, hid, packed, total_ref, sems,
+    left_hbm, hid, hid_hbm, pack_hbm, total_hbm,
+    feat, w, picks, counts, left, packed, total_ref, sems,
 ):
     copies = Copies(sems)
     rows, width = feat.shape
@@ -154,7 +159,7 @@
     left[:, relations * width :] = own
     for i, at in enumerate(chunks):
         sums = dot(adj[at, :rows], own) + dot(adj[at, rows:], got)
-        avg = (sums * wide(norm[at, :], width)).astype(bf16)
+        avg = (sums * norm_of(norm[at, :], width)).astype(bf16)
         left[:, 2 * i * width : (2 * i + 1) * width] = avg[:rows]
         left[:, (2 * i + 1) * width : (2 * i + 2) * width] = avg[rows:]
     out = [copies.start(left, left_hbm)]
@@ -178,29 +183,27 @@
 
 
 def second_kernel(
-    block, me_ref, got_ref, adj, norm, back_hbm, hid_hbm, w_hbm, self_hbm, label_hbm, total_hbm,
-    logit_hbm, keep_hbm, send_hbm, grad_hbm, local_hbm, out_hbm,
-    back, hid, w, selfs, label, total, logit, turned, blocks, grad_ref, spreads,
-    local_ref, packed, sems,
+    block, me_ref, got_ref, adj, norm, hid, back_hbm, w_hbm, self_hbm, label_hbm, total_hbm,
+    logit_hbm, keep_hbm, send_hbm, grad_hbm, spread_hbm, out_hbm,
+    back, w, selfs, label, total, logit, turned, blocks, grad_ref, spreads,
+    packed, sems,
 ):
     copies = Copies(sems)
     rows, width = hid.shape
     relations, classes, _ = w.shape
     chunks = [slice(r * rows, (r + 2) * rows) for r in range(0, relations, 2)]
-    near = [copies.start(hid_hbm, hid)]
     w_in = []
     for i in range(len(chunks)):
         w_in.append(copies.start(w_hbm.at[2 * i : 2 * i + 2], w.at[2 * i : 2 * i + 2]))
     small = [copies.start(a, b) for a, b in ((self_hbm, selfs), (label_hbm, label), (total_hbm, total))]
-    back_in = copies.start(back_hbm, back)
-    wait_all(near)
+    back_in = copies.start(back_hbm.at[rows:, :], back)
     own = hid[...]
     got = got_ref[...]
     logits = None
     turned[relations * width :, :] = own.T.astype(turned.dtype)
     for i, at in enumerate(chunks):
         sums = dot(adj[at, :rows], own) + dot(adj[at, rows:], got)
-        avg = (sums * wide(norm[at, :], width)).astype(bf16)
+        avg = (sums * norm_of(norm[at, :], width)).astype(bf16)
         w_in[i].wait()
         part = dot_nt(w[2 * i], avg[:rows]) + dot_nt(w[2 * i + 1], avg[rows:])
         logits = part if logits is None else logits + part
@@ -227,8 +230,11 @@
     out.append(copies.start(grad_ref, grad_hbm))
     for r in range(relations):
         at = slice(r * rows, (r + 1) * rows)
-        spread = dot(grad, w[r]) * wide(norm[at, :], width)
+        spread = dot(grad, w[r]) * norm_of(norm[at, :], width)
         spreads[at, :] = spread.astype(bf16)
+        if r % 4 == 3:
+            part = slice((r - 3) * rows, (r + 1) * rows)
+            out.append(copies.start(spreads.at[part, :], spread_hbm.at[part, :]))
     slots = packed.shape[0]
     first = local.astype(bf16).astype(f32)
     second = (local - first).astype(bf16).astype(f32)
@@ -236,10 +242,8 @@
     lane = iota((slots, EXTRA), 1)
     packed[:, width:] = jnp.where(lane < 32, first, jnp.where(lane < 64, second, third)).astype(bf16)
     back_in.wait()
-    packed[:, :width] = dot(back[rows:, :], spreads[...]).astype(bf16)
+    packed[:, :width] = dot(back[...], spreads[...]).astype(bf16)
     out.append(copies.start(packed, out_hbm))
-    local_ref[...] = dot(back[:rows, :], spreads[...]) + dot(grad, selfs[...])
-    out.append(copies.start(local_ref, local_hbm))
     wait_all(out)
 
 
@@ -274,6 +278,23 @@
     loss_ref[...] = loss / total[0:1, 0:1]
 
 
+def local_kernel(
+    keep_hbm, grad_hbm, back_hbm, spread_hbm, self_hbm, keep_ref, grad_ref, local_hbm,
+    back, spreads, selfs, local, sems,
+):
+    copies = Copies(sems)
+    rows = local.shape[0]
+    first = copies.start(grad_hbm, grad_ref), copies.start(self_hbm, selfs)
+    brought = copies.start(keep_hbm, keep_ref)
+    ins = copies.start(back_hbm.at[:rows, :], back), copies.start(spread_hbm, spreads)
+    wait_all(first)
+    own = dot(grad_ref[...], selfs[...])
+    wait_all(ins)
+    local[...] = dot(back[...], spreads[...]) + own
+    copies.start(local, local_hbm).wait()
+    brought.wait()
+
+
 def bring_kernel(*refs):
     count = len(refs) // 2
     copies = Copies(refs[-1])
@@ -295,16 +316,19 @@
         return [p for p in here if p >> bit & 1], [p for p in here if not p >> bit & 1]
 
 
-def colours_of(bits, rows):
+ORDERS_ONE = [[0, 1, 3, 2], [1, 2, 0, 3], [2, 0, 1, 3]]
+ORDERS_TWO = [[0, 1, 3, 2], [2, 0, 1, 3], [2, 0, 1, 3]]
+
+
+def colours_of(bits, rows, orders):
     tiles = rows // 16
     last = list(range(4, bits))
-    orders = [[0, 2, 1, 3] + last, [1, 0, 2, 3] + last, [2, 1, 3, 0] + last]
     third = tiles // 3
     sizes = [tiles - 2 * third, third, third]
     out, at = [], 0
     for size, order in zip(sizes, orders):
         if size:
-            out.append(Colour(at * 16, size * 16, order))
+            out.append(Colour(at * 16, size * 16, order + last))
         at += size
     return out
 
@@ -329,14 +353,30 @@
             out[j] = (kept[k] + got[k].astype(f32)).astype(out.dtype)
 
 
-def last_kernel(colours, block, *refs):
+def join_kernel(colours, stage, *refs):
+    count = len(colours)
+    ins, (sent, stay) = refs[: 2 * count], refs[2 * count :]
+    at = 0
+    for i, colour in enumerate(colours):
+        got, kept = ins[2 * i], ins[2 * i + 1]
+        here = colour.places(stage)
+        for places, out in zip(colour.split(stage), (sent, stay)):
+            k = here.index(places[0])
+            value = (kept[k] + got[k].astype(f32)).astype(out.dtype)
+            out[at : at + colour.size, :] = value
+        at += colour.size
+
+
+def last_kernel(groups, block, *refs):
     out = refs[-1]
-    for i, colour in enumerate(colours):
-        got, kept = refs[2 * i], refs[2 * i + 1]
-        size = min(colour.size, block - colour.start)
-        if size > 0:
-            value = kept[0] + got[0].astype(f32)
-            out[colour.start : colour.start + size, :] = value[:size]
+    for i, group in enumerate(groups):
+        value = refs[2 * i + 1][...] + refs[2 * i][...].astype(f32)
+        at = 0
+        for colour in group:
+            size = min(colour.size, block - colour.start)
+            if size > 0:
+                out[colour.start : colour.start + size, :] = value[at : at + size]
+            at += colour.size
 
 
 def across(value, bit):
@@ -372,20 +412,37 @@
     )
 
 
+def groups_of(colours):
+    last = {}
+    for i, colour in enumerate(colours):
+        last.setdefault(colour.order[-1], []).append(i)
+    return list(last.values())
+
+
 def scatter_sum(colours, block, parts):
     bits = len(colours[0].order)
-    ends = []
     states = [list(parts[2 * i : 2 * i + 2]) for i in range(len(colours))]
-    for stage in range(bits):
+    for stage in range(bits - 1):
         for i, colour in enumerate(colours):
             sent, kept = states[i]
             got = across(sent, colour.order[stage])
-            if stage + 1 < bits:
+            if stage + 2 < bits:
                 states[i] = add_stage(colour, stage + 1, got, kept)
             else:
-                ends += [got, kept]
+                states[i] = [got, kept]
+    ends, groups = [], []
+    for group in groups_of(colours):
+        members = [colours[i] for i in group]
+        ins = [x for i in group for x in states[i]]
+        shape = (sum(c.size for c in members), ins[0].shape[2])
+        sent, kept = call(
+            functools.partial(join_kernel, members, bits - 1), [(shape, bf16), (shape, f32)], ins,
+            "v" * len(ins), "vv", flops=shape[0] * 1000, moved=shape[0] * 9000, vmem=4,
+        )
+        ends += [across(sent, members[0].order[-1]), kept]
+        groups.append(members)
     return call(
-        functools.partial(last_kernel, colours, block), [((block, ends[0].shape[2]), f32)], ends,
+        functools.partial(last_kernel, groups, block), [((block, ends[0].shape[1]), f32)], ends,
         "v" * len(ends), "v", flops=block * 1000, moved=block * 5000, vmem=4,
     )[0]
 
@@ -413,7 +470,8 @@
     block = (relations + 1) * width // peers
     padded = -(-block // 16) * 16
     bits = peers.bit_length() - 2
-    colours = colours_of(bits, padded)
+    shares_one = colours_of(bits, padded, ORDERS_ONE)
+    shares_two = colours_of(bits, padded, ORDERS_TWO)
     w_two = jnp.swapaxes(w_two, 1, 2)
     self_two = self_two.T
 
@@ -439,17 +497,18 @@
     got_one = exchange(packed)
     adj, norm, back = call(
         graph_kernel,
-        [((all_rows, table), bf16), ((all_rows, EXTRA), f32), ((table, all_rows), bf16)],
+        [((all_rows, table), bf16), ((all_rows, EXTRA), bf16), ((table, all_rows), bf16)],
         (edge_src, edge_dst), "hh", near + near + "h", [edge_vm] * 2 + [back_vm], 3,
         flops=4 * all_rows * 256 * table, moved=5 << 20,
     )
-    left_one, hidden, packed, total = call(
+    left_one, hidden_near, hidden, packed, total = call(
         first_kernel,
-        [((rows, deep), bf16), ((rows, width), bf16), ((boundary, width), bf16), ((8, EXTRA), f32)],
+        [((rows, deep), bf16)] + [((rows, width), bf16)] * 2
+        + [((boundary, width), bf16), ((8, EXTRA), f32)],
         (adj, norm, got_one, features, w_one.reshape(deep, width), picks, send_count),
-        near + near + "vhhhh", "hhhh",
-        [ own_vm, vm((deep, width), bf16), picks_vm, counts_vm, left_vm,
-            own_vm, vm((boundary, width), bf16), total_vm,
+        near + near + "vhhhh", "h" + near + "hhh",
+        [
+            own_vm, vm((deep, width), bf16), picks_vm, counts_vm, left_vm, vm((boundary, width), bf16), total_vm,
         ],
         10,
         flops=2 * all_rows * width * (table + width), moved=10 << 20,
@@ -460,27 +519,33 @@
         [left_vm, turned_vm, blocks_vm], 5, flops=1 << 30, moved=5 << 20,
     )
     other_one = to_pair(send_one)
-    logits, keep_two, send_two, grad_logits, local, outgoing = call(
+    logits, keep_two, send_two, grad_logits, spread, outgoing = call(
         functools.partial(second_kernel, block),
         [((classes, rows), f32)] + turn_outs
-        + [((rows, classes), bf16), ((rows, width), f32), ((boundary, width + EXTRA), bf16)],
-        (me, got_two, adj, norm, back, hidden, w_two, self_two, label_row, total), "sv" + near + near + "hhhhhh", "hhhhhh",
+        + [((rows, classes), bf16), ((all_rows, width), bf16), ((boundary, width + EXTRA), bf16)],
+        (me, got_two, adj, norm, hidden_near, back, w_two, self_two, label_row, total),
+        "sv" + near * 3 + "hhhhh", "hhhhhh",
         [
-            back_vm, own_vm, vm(w_two.shape, bf16),
+            vm((boundary, all_rows), bf16), vm(w_two.shape, bf16),
             vm(self_two.shape, bf16), vm((1, rows), jnp.int32), total_vm, vm((classes, rows), f32),
             turned_vm, blocks_vm, vm((rows, classes), bf16), vm((all_rows, width), bf16),
-            vm((rows, width), f32), packed_vm,
+            packed_vm,
         ],
-        1 + relations // 2 + 4 + 6,
+        relations // 2 + 4 + 5 + relations // 4,
         flops=8 * all_rows * width * width, moved=16 << 20,
     )
     other_two, other_logits = to_pair(send_two), to_pair(grad_logits)
     returned = exchange(outgoing)
-    keep_two, grad_logits = call(
-        bring_kernel, [turn_outs[0], ((rows, classes), bf16)], (keep_two, grad_logits), "hh", "VV", (), 2,
-        flops=1 << 20, moved=3 << 20, vmem=16,
-    )
-    parts_two = product(colours, keep_two, other_two, grad_logits, other_logits, "Hv")
+    keep_two, grad_logits, local = call(
+        local_kernel, [turn_outs[0], ((rows, classes), bf16), ((rows, width), f32)],
+        (keep_two, grad_logits, back, spread, self_two), "hhhhh", "VVh",
+        [
+            vm((rows, all_rows), bf16), vm((all_rows, width), bf16), vm(self_two.shape, bf16),
+            vm((rows, width), f32),
+        ], 6,
+        flops=1 << 20, moved=3 << 20,
+    )
+    parts_two = product(shares_two, keep_two, other_two, grad_logits, other_logits, "Hv")
     grad_pre, loss = call(
         grad_pre_kernel, [((rows, width), bf16), ((1, 1), f32)],
         (returned, parts_two[0], local, hidden, picks, send_count, total), "vhhhhhh", "Vv",
@@ -492,9 +557,9 @@
         bring_kernel, turn_outs, (keep_one, other_one), "hh", "VV", (), 2,
         flops=1 << 20, moved=5 << 20,
     )
-    parts_one = product(colours, keep_one, other_one, grad_pre, other_pre, "vv")
-    grad_two = scatter_sum(colours, block, parts_two)
-    grad_one = scatter_sum(colours, block, parts_one)
+    parts_one = product(shares_one, keep_one, other_one, grad_pre, other_pre, "vv")
+    grad_two = scatter_sum(shares_two, block, parts_two)
+    grad_one = scatter_sum(shares_one, block, parts_one)
     return (logits.T, loss.reshape(()), grad_one, grad_two)
 
 

time: 124 us -> 124 us (level)
  starting transfers between devices: 38.1 us -> 33 us
  waiting for transfers between devices: 44.4 us -> 48.7 us
  Pallas kernels: 35.1 us -> 36.9 us
    ppermute x24 -> x22, waiting for transfers between devices: 23.2 us -> 30.3 us  [across(): return lax.ppermute(value, 'dom', [(i, i ^ 2 << bit) for i in range(size)])]
    ppermute x24 -> x22, starting transfers between devices: 24.6 us -> 19.5 us  [across(): return lax.ppermute(value, 'dom', [(i, i ^ 2 << bit) for i in range(size)])]
    all_to_all x3, waiting for transfers between devices: 21 us -> 18.4 us  [exchange(): got = lax.all_to_all(cut, 'dom', split_axis=0, concat_axis=0, tiled=True)]
    pallas_call x30 -> x28, Pallas kernels: 35.1 us -> 36.9 us  [call(): pl.pallas_call(body, out_shape=[kept[c](s, d) if c in kept else jax.Shape...]
  transfers between devices with their start and end apart: 31 -> 29, of which waited for: 15 -> 14; matrix products, arithmetic and copies ran while one was open for 4% -> 3% of each run, Pallas kernels for 15% -> 16%
where the time goes in v2:
time: 124 us
  waiting for transfers between devices  48.7 us (39%)
  Pallas kernels  36.9 us (30%)
  starting transfers between devices  33 us (27%)
  local copies, waits for them, and re-layouts  4.33 us (3%)
    pallas_call x28, Pallas kernels, call(): pl.pallas_call(body, out_shape=[kept[c](s, d) if c in kept else jax.Shape...  36.9 us
    ppermute x22, waiting for transfers between devices, across(): return lax.ppermute(value, 'dom', [(i, i ^ 2 << bit) for i in range(size)])  30.3 us
    ppermute x22, starting transfers between devices, across(): return lax.ppermute(value, 'dom', [(i, i ^ 2 << bit) for i in range(size)])  19.5 us
    all_to_all x3, waiting for transfers between devices, exchange(): got = lax.all_to_all(cut, 'dom', split_axis=0, concat_axis=0, tiled=True)  18.4 us
    all_to_all x3, starting transfers between devices, exchange(): got = lax.all_to_all(cut, 'dom', split_axis=0, concat_axis=0, tiled=True)  12.7 us
    unnamed x9, local copies, waits for them, and re-layouts  4.33 us
  transfers between devices with their start and end apart: 29, of which 14 were waited for; matrix products, arithmetic and copies ran while one was open for 3% of the time, Pallas kernels for 16%

profile of v2, /device:TPU:0, one launch (start us, length us, event | category | flops | bytes accessed | tf_op | source)
XLA Modules:
  0.0 123.8 jit_solution(6486272027818415774)
XLA Ops:
  0.6 2.0 %shard_map.121 = bf16[256,640]{1,0:T(8,128)(2,1)} custom-call(bf16[256,512]{1,0:T(8,128)(2,1)} %feat_hbm.3, s32[8,32]{1,0:T(8,128)} %bitcast.25, s32[1,32]{1,0:T(1,128)} %count_hbm.5, s32[1,256]{1,0:T(1,128)} %bitcast.28), custom_call_target="tpu_custom_call" | custom-call | flops 67108864 | bytes 600000 | tf_op jit(solution)/shard_map/pallas_call | solution.py:40
  2.6 7.3 %all-to-all-start = ((bf16[32,8,640]{2,1,0:T(8,128)(2,1)}), bf16[32,8,640]{2,1,0:T(8,128)(2,1)S(1)}, u32[]{:S(2)}, u32[]{:S(2)}) async-start(bf16[32,8,640]{2,1,0:T(8,128)(2,1)} %bitcast.4), calls=%async_computation | async-start | bytes 655360 | tf_op jit(solution)/shard_map/all_to_all | solution.py:454
  10.0 5.7 %shard_map.120 = (bf16[2048,512]{1,0:T(8,128)(2,1)S(1)}, bf16[2048,128]{1,0:T(8,128)(2,1)S(1)}, bf16[512,2048]{1,0:T(8,128)(2,1)}) custom-call(s32[8,2,256]{2,1,0:T(2,128)} %src_hbm.1, s32[8,2,256]{2,1,0:T(2,128)} %dst_hbm.1), custom_call_target="tpu_custom_call" | custom-call | flops 1073741824 | bytes 5242880 | tf_op jit(solution)/shard_map/pallas_call | solution.py:40
  15.6 6.4 %all-to-all-done = bf16[32,8,640]{2,1,0:T(8,128)(2,1)S(1)} async-done(((bf16[32,8,640]{2,1,0:T(8,128)(2,1)}), bf16[32,8,640]{2,1,0:T(8,128)(2,1)S(1)}, u32[]{:S(2)}, u32[]{:S(2)}) %all-to-all-start) | async-done | bytes 327712 | tf_op jit(solution)/shard_map/all_to_all | solution.py:454
  22.0 5.1 %shard_map.122 = (bf16[256,4608]{1,0:T(8,128)(2,1)}, bf16[256,512]{1,0:T(8,128)(2,1)S(1)}, bf16[256,512]{1,0:T(8,128)(2,1)}, bf16[256,512]{1,0:T(8,128)(2,1)}, f32[8,128]{1,0:T(8,128)}) custom-call(bf16[2048,512]{1,0:T(8,128)(2,1)S(1)} %get-tuple-element.71.adj, bf16[2048,128]{1,0:T(8,128)(2,1)S(1)} %get-tuple-element.72.norm, ...), custom_call_target="tpu_custom_call" | custom-call | flops 2147483648 | bytes 10485760 | tf_op jit(solution)/shard_map/pallas_call | solution.py:40
  27.2 2.6 %all-to-all-start.1 = ((bf16[32,8,512]{2,1,0:T(8,128)(2,1)}), bf16[32,8,512]{2,1,0:T(8,128)(2,1)S(1)}, u32[]{:S(2)}, u32[]{:S(2)}) async-start(bf16[32,8,512]{2,1,0:T(8,128)(2,1)} %bitcast.24), calls=%async_computation.1 | async-start | bytes 524288 | tf_op jit(solution)/shard_map/all_to_all | solution.py:454
  29.8 4.3 %copy.15 = bf16[8,512,349]{1,2,0:T(8,128)(2,1)} copy(bf16[8,512,349]{1,0,2:T(8,128)(2,1)} %param.11) | data formatting | bytes 5718016 | tf_op args[2]
  34.1 6.3 %all-to-all-done.1 = bf16[32,8,512]{2,1,0:T(8,128)(2,1)S(1)} async-done(((bf16[32,8,512]{2,1,0:T(8,128)(2,1)}), bf16[32,8,512]{2,1,0:T(8,128)(2,1)S(1)}, u32[]{:S(2)}, u32[]{:S(2)}) %all-to-all-start.1) | async-done | bytes 262176 | tf_op jit(solution)/shard_map/all_to_all | solution.py:454
  40.3 7.9 %shard_map.123 = (f32[349,256]{1,0:T(8,128)}, bf16[16,144,256]{2,1,0:T(8,128)(2,1)}, bf16[16,144,256]{2,1,0:T(8,128)(2,1)}, bf16[256,349]{1,0:T(8,128)(2,1)}, bf...) custom-call(s32[1]{0:T(128)} %bitcast.me_ref, bf16[256,512]{1,0:T(8,128)(2,1)S(1)} %bitcast.20, ...), custom_call_target="tpu_custom_call" | custom-call | flops 4294967296 | bytes 16777216 | tf_op jit(solution)/shard_map/pallas_call | solution.py:40
  48.2 0.1 collective-permute-start
  48.3 0.0 copy-start.1
  48.3 3.4 %shard_map.127 = (bf16[16,144,256]{2,1,0:T(8,128)(2,1)}, bf16[16,144,256]{2,1,0:T(8,128)(2,1)}) custom-call(s32[1]{0:T(128)} %bitcast.me_ref, bf16[256,4608]{1,0:T(8,128)(2,1)} %get-tuple-element.89.left_hbm), custom_call_target="tpu_custom_call" | custom-call | flops 1073741824 | bytes 5242880 | tf_op jit(solution)/shard_map/pallas_call | solution.py:40
  51.8 0.6 collective-permute-start.2
  52.3 2.8 %all-to-all-start.2 = ((bf16[32,8,640]{2,1,0:T(8,128)(2,1)}), bf16[32,8,640]{2,1,0:T(8,128)(2,1)S(1)}, u32[]{:S(2)}, u32[]{:S(2)}) async-start(bf16[32,8,640]{2,1,0:T(8,128)(2,1)} %bitcast.12), calls=%async_computation.2 | async-start | bytes 655360 | tf_op jit(solution)/shard_map/all_to_all | solution.py:454
  55.1 0.1 collective-permute-start.1
  55.2 4.0 %shard_map.124 = (bf16[16,144,256]{2,1,0:T(8,128)(2,1)S(1)}, bf16[256,349]{1,0:T(8,128)(2,1)S(1)}, f32[256,512]{1,0:T(8,128)}) custom-call(bf16[16,144,256]{2,1,0:T(8,128)(2,1)} %get-tuple-element.79.keep_hbm, bf16[256,349]{1,0:T(8,128)(2,1)} %get-tuple-element.80.grad_hbm, bf16[512,2048]{1,0:T(8,128)(2,1)} %get-tuple-element.75.back_hbm, ...), custom_call_target="tpu_custom_call" | custom-call | flops 1048576 | bytes 3145728 | tf_op jit(solution)/shard_map/pallas_call | solution.py:40
  59.2 1.9 %shard_map.125 = (bf16[8,48,349]{2,1,0:T(8,128)(2,1)}, f32[8,48,349]{2,1,0:T(8,128)S(1)}, bf16[8,48,349]{2,1,0:T(8,128)(2,1)}, f32[8,48,349]{2,1,0:T(8,128)S(1)}...) custom-call(bf16[16,144,256]{2,1,0:T(8,128)(2,1)S(1)} %get-tuple-element.82.keep_ref, ...), custom_call_target="tpu_custom_call" | custom-call | flops 823394304 | bytes 7077888 | tf_op jit(solution)/shard_map/pallas_call | solution.py:40
  61.2 5.8 %all-to-all-done.2 = bf16[32,8,640]{2,1,0:T(8,128)(2,1)S(1)} async-done(((bf16[32,8,640]{2,1,0:T(8,128)(2,1)}), bf16[32,8,640]{2,1,0:T(8,128)(2,1)S(1)}, u32[]{:S(2)}, u32[]{:S(2)}) %all-to-all-start.2) | async-done | bytes 327712 | tf_op jit(solution)/shard_map/all_to_all | solution.py:454
  66.9 1.7 %shard_map.126 = (bf16[256,512]{1,0:T(8,128)(2,1)S(1)}, f32[1,1]{1,0:T(1,128)}) custom-call(bf16[256,640]{1,0:T(8,128)(2,1)S(1)} %bitcast.18, bf16[8,48,349]{2,1,0:T(8,128)(2,1)} %get-tuple-element.85.after_ref, f32[256,512]{1,0:T(8,128)} %get-tuple-element.86.local_hbm, bf16[256,512]{1,0:T(8,128)(2,1)} %get-tuple-element.87.hid_hbm, s32[8,32]{1,0:T(8,128)} %bitcast.27, ...), custom_call_target="tpu_custom_call" | custom-call | flops 67108864 | bytes 2097152 | tf_op jit(solution)/shard_map/pallas_call | solution.py:40
  68.7 0.1 collective-permute-start.3
  68.7 1.6 %shard_map.128 = (bf16[16,144,256]{2,1,0:T(8,128)(2,1)S(1)}, bf16[16,144,256]{2,1,0:T(8,128)(2,1)S(1)}) custom-call(bf16[16,144,256]{2,1,0:T(8,128)(2,1)} %get-tuple-element.90.refs_0_, bf16[16,144,256]{2,1,0:T(8,128)(2,1)} %collective-permute-done.2.refs_1_), custom_call_target="tpu_custom_call" | custom-call | flops 1048576 | bytes 5242880 | tf_op jit(solution)/shard_map/pallas_call | solution.py:40
  70.4 0.0 copy-start
  70.4 1.4 %shard_map.129 = (bf16[8,48,512]{2,1,0:T(8,128)(2,1)S(1)}, f32[8,48,512]{2,1,0:T(8,128)S(1)}, bf16[8,48,512]{2,1,0:T(8,128)(2,1)S(1)}, f32[8,48,512]{2,1,0:T(8,1...) custom-call(bf16[16,144,256]{2,1,0:T(8,128)(2,1)S(1)} %get-tuple-element.92.keep_ref, ...), custom_call_target="tpu_custom_call" | custom-call | flops 1207959552 | bytes 7077888 | tf_op jit(solution)/shard_map/pallas_call | solution.py:40
  71.8 0.8 collective-permute-start.8
  72.6 0.7 collective-permute-start.11
  73.3 0.6 collective-permute-start.4
  73.9 1.7 %collective-permute-start.19 = (bf16[8,48,349]{2,1,0:T(8,128)(2,1)S(1)}, bf16[8,48,349]{2,1,0:T(8,128)(2,1)S(1)}, u32[]{:S(2)}, u32[]{:S(2)}) collective-permute-start(bf16[8,48,349]{2,1,0:T(8,128)(2,1)S(1)} %copy-done.3), channel_id=1, source_target_pairs={{0,8},{1,9},{2,10},{3,11},{4,12},{5,13},{6,14},{7,15},{8,0},{9,1},... | collective-permute-start | bytes 804104 | tf_op jit(solution)/shard_map/ppermute | solution.py:384
  75.6 0.3 collective-permute-start.22
  75.9 7.5 %collective-permute-done.8.got = bf16[8,48,512]{2,1,0:T(8,128)(2,1)S(1)} collective-permute-done((bf16[8,48,512]{2,1,0:T(8,128)(2,1)S(1)}, bf16[8,48,512]{2,1,0:T(8,128)(2,1)S(1)}, u32[]{:S(2)}, u32[]{:S(2)}) %collective-permute-start.8) | collective-permute-done | bytes 393248 | tf_op jit(solution)/shard_map/ppermute | solution.py:384
  83.4 0.2 collective-permute-start.15
  83.6 0.1 shard_map.133
  83.7 0.9 collective-permute-done.11.got
  84.6 0.7 collective-permute-start.9
  85.3 0.1 shard_map.135
  85.4 1.1 collective-permute-start.12
  86.5 0.1 shard_map.130
  86.6 4.4 %collective-permute-done.19.got = bf16[8,48,349]{2,1,0:T(8,128)(2,1)S(1)} collective-permute-done((bf16[8,48,349]{2,1,0:T(8,128)(2,1)S(1)}, bf16[8,48,349]{2,1,0:T(8,128)(2,1)S(1)}, u32[]{:S(2)}, u32[]{:S(2)}) %collective-permute-start.19) | collective-permute-done | bytes 268064 | tf_op jit(solution)/shard_map/ppermute | solution.py:384
  91.0 1.3 %collective-permute-start.5 = (bf16[4,48,512]{2,1,0:T(8,128)(2,1)S(1)}, bf16[4,48,512]{2,1,0:T(8,128)(2,1)S(1)}, u32[]{:S(2)}, u32[]{:S(2)}) collective-permute-start(bf16[4,48,512]{2,1,0:T(8,128)(2,1)S(1)} %get-tuple-element.97), channel_id=1, source_target_pairs={{0,4},{1,5},{2,6},{3,7},{4,0},{5,1},{6,2},{7,3},{8,12},{9,13},{10,... | collective-permute-start | bytes 589832 | tf_op jit(solution)/shard_map/ppermute | solution.py:384
  92.2 0.1 shard_map.142
  92.3 5.0 %collective-permute-done.22.got = bf16[8,48,349]{2,1,0:T(8,128)(2,1)S(1)} collective-permute-done((bf16[8,48,349]{2,1,0:T(8,128)(2,1)S(1)}, bf16[8,48,349]{2,1,0:T(8,128)(2,1)S(1)}, u32[]{:S(2)}, u32[]{:S(2)}) %collective-permute-start.22) | collective-permute-done | bytes 268064 | tf_op jit(solution)/shard_map/ppermute | solution.py:384
  97.3 0.9 collective-permute-start.20
  98.2 0.1 shard_map.144
  98.3 1.2 collective-permute-start.23
  99.4 0.1 shard_map.139
  99.5 1.2 %collective-permute-done.9.got = bf16[4,48,512]{2,1,0:T(8,128)(2,1)S(1)} collective-permute-done((bf16[4,48,512]{2,1,0:T(8,128)(2,1)S(1)}, bf16[4,48,512]{2,1,0:T(8,128)(2,1)S(1)}, u32[]{:S(2)}, u32[]{:S(2)}) %collective-permute-start.9) | collective-permute-done | bytes 196640 | tf_op jit(solution)/shard_map/ppermute | solution.py:384
  100.7 1.3 %collective-permute-start.16 = (bf16[4,48,349]{2,1,0:T(8,128)(2,1)S(1)}, bf16[4,48,349]{2,1,0:T(8,128)(2,1)S(1)}, u32[]{:S(2)}, u32[]{:S(2)}) collective-permute-start(bf16[4,48,349]{2,1,0:T(8,128)(2,1)S(1)} %get-tuple-element.118), channel_id=1, source_target_pairs={{0,4},{1,5},{2,6},{3,7},{4,0},{5,1},{6,2},{7,3},{8,12},{9,13},{10,... | collective-permute-start | bytes 402056 | tf_op jit(solution)/shard_map/ppermute | solution.py:384
  102.0 0.3 collective-permute-start.10
  102.4 1.5 %collective-permute-start.13 = (bf16[2,48,512]{2,1,0:T(8,128)(2,1)S(1)}, bf16[2,48,512]{2,1,0:T(8,128)(2,1)S(1)}, u32[]{:S(2)}, u32[]{:S(2)}) collective-permute-start(bf16[2,48,512]{2,1,0:T(8,128)(2,1)S(1)} %get-tuple-element.113), channel_id=1, source_target_pairs={{0,4},{1,5},{2,6},{3,7},{4,0},{5,1},{6,2},{7,3},{8,12},{9,13},{10,... | collective-permute-start | bytes 294920 | tf_op jit(solution)/shard_map/ppermute | solution.py:384
  103.9 0.3 collective-permute-start.6
  104.2 1.5 %collective-permute-done.23.got = bf16[4,48,349]{2,1,0:T(8,128)(2,1)S(1)} collective-permute-done((bf16[4,48,349]{2,1,0:T(8,128)(2,1)S(1)}, bf16[4,48,349]{2,1,0:T(8,128)(2,1)S(1)}, u32[]{:S(2)}, u32[]{:S(2)}) %collective-permute-start.23) | collective-permute-done | bytes 134048 | tf_op jit(solution)/shard_map/ppermute | solution.py:384
  105.8 1.3 %collective-permute-start.21 = (bf16[2,48,349]{2,1,0:T(8,128)(2,1)S(1)}, bf16[2,48,349]{2,1,0:T(8,128)(2,1)S(1)}, u32[]{:S(2)}, u32[]{:S(2)}) collective-permute-start(bf16[2,48,349]{2,1,0:T(8,128)(2,1)S(1)} %get-tuple-element.128), channel_id=1, source_target_pairs={{0,4},{1,5},{2,6},{3,7},{4,0},{5,1},{6,2},{7,3},{8,12},{9,13},{10,... | collective-permute-start | bytes 201032 | tf_op jit(solution)/shard_map/ppermute | solution.py:384
  107.1 0.3 collective-permute-done.16.got
  107.4 1.3 %collective-permute-start.24 = (bf16[2,48,349]{2,1,0:T(8,128)(2,1)S(1)}, bf16[2,48,349]{2,1,0:T(8,128)(2,1)S(1)}, u32[]{:S(2)}, u32[]{:S(2)}) collective-permute-start(bf16[2,48,349]{2,1,0:T(8,128)(2,1)S(1)} %get-tuple-element.134), channel_id=1, source_target_pairs={{0,4},{1,5},{2,6},{3,7},{4,0},{5,1},{6,2},{7,3},{8,12},{9,13},{10,... | collective-permute-start | bytes 201032 | tf_op jit(solution)/shard_map/ppermute | solution.py:384
  108.8 0.5 collective-permute-start.17
  109.3 0.2 collective-permute-done.13.refs_2_
  109.5 2.3 %collective-permute-start.14 = (bf16[96,512]{1,0:T(8,128)(2,1)S(1)}, bf16[96,512]{1,0:T(8,128)(2,1)S(1)}, u32[]{:S(2)}, u32[]{:S(2)}) collective-permute-start(bf16[96,512]{1,0:T(8,128)(2,1)S(1)} %get-tuple-element.115), channel_id=1, source_target_pairs={{0,16},{1,17},{2,18},{3,19},{4,20},{5,21},{6,22},{7,23},{8,24},{9,... | collective-permute-start | bytes 294920 | tf_op jit(solution)/shard_map/ppermute | solution.py:384
  111.9 0.7 collective-permute-start.25
  112.6 0.5 collective-permute-done.6.refs_0_
  113.1 0.4 collective-permute-start.7
  113.5 4.7 %collective-permute-done.17.refs_0_ = bf16[2,48,349]{2,1,0:T(8,128)(2,1)S(1)} collective-permute-done((bf16[2,48,349]{2,1,0:T(8,128)(2,1)S(1)}, bf16[2,48,349]{2,1,0:T(8,128)(2,1)S(1)}, u32[]{:S(2)}, u32[]{:S(2)}) %collective-permute-start.17) | collective-permute-done | bytes 67040 | tf_op jit(solution)/shard_map/ppermute | solution.py:384
  118.3 0.1 collective-permute-start.18
  118.4 3.9 %collective-permute-done.18.refs_0_ = bf16[48,349]{1,0:T(8,128)(2,1)S(1)} collective-permute-done((bf16[48,349]{1,0:T(8,128)(2,1)S(1)}, bf16[48,349]{1,0:T(8,128)(2,1)S(1)}, u32[]{:S(2)}, u32[]{:S(2)}) %collective-permute-start.18) | collective-permute-done | bytes 33536 | tf_op jit(solution)/shard_map/ppermute | solution.py:384
  122.3 0.7 shard_map.147
  123.1 0.7 shard_map.138
  (31 shorter events, 0.3 us)
Async XLA Ops:
  2.6 19.4 %all-to-all-start = ((bf16[32,8,640]{2,1,0:T(8,128)(2,1)}), bf16[32,8,640]{2,1,0:T(8,128)(2,1)S(1)}, u32[]{:S(2)}, u32[]{:S(2)}) async-start(bf16[32,8,640]{2,1,0:T(8,128)(2,1)} %bitcast.4), calls=%async_computation | async-start | bytes 655360 | tf_op jit(solution)/shard_map/all_to_all | solution.py:454
  27.2 13.2 %all-to-all-start.1 = ((bf16[32,8,512]{2,1,0:T(8,128)(2,1)}), bf16[32,8,512]{2,1,0:T(8,128)(2,1)S(1)}, u32[]{:S(2)}, u32[]{:S(2)}) async-start(bf16[32,8,512]{2,1,0:T(8,128)(2,1)} %bitcast.24), calls=%async_computation.1 | async-start | bytes 524288 | tf_op jit(solution)/shard_map/all_to_all | solution.py:454
  48.2 11.0 %collective-permute-start = (bf16[16,144,256]{2,1,0:T(8,128)(2,1)}, bf16[16,144,256]{2,1,0:T(8,128)(2,1)S(1)}, u32[]{:S(2)}, u32[]{:S(2)}) collective-permute-start(bf16[16,144,256]{2,1,0:T(8,128)(2,1)} %get-tuple-element.83), channel_id=1, source_target_pairs={{0,1},{1,0},{2,3},{3,2},{4,5},{5,4},{6,7},{7,6},{8,9},{9,8},{10,11... | collective-permute-start | bytes 3538952 | tf_op jit(solution)/shard_map/ppermute | solution.py:389
  48.3 6.8 %copy-start.1 = (bf16[256,349]{1,0:T(8,128)(2,1)S(1)}, bf16[256,349]{1,0:T(8,128)(2,1)}, u32[]{:S(2)}) copy-start(bf16[256,349]{1,0:T(8,128)(2,1)} %get-tuple-element.80.grad_hbm) | copy-start | bytes 536068
  51.8 17.0 %collective-permute-start.2 = (bf16[16,144,256]{2,1,0:T(8,128)(2,1)}, bf16[16,144,256]{2,1,0:T(8,128)(2,1)}, u32[]{:S(2)}, u32[]{:S(2)}) collective-permute-start(bf16[16,144,256]{2,1,0:T(8,128)(2,1)} %get-tuple-element.91), channel_id=1, source_target_pairs={{0,1},{1,0},{2,3},{3,2},{4,5},{5,4},{6,7},{7,6},{8,9},{9,8},{10,11... | collective-permute-start | bytes 3538952 | tf_op jit(solution)/shard_map/ppermute | solution.py:389
  52.3 14.6 %all-to-all-start.2 = ((bf16[32,8,640]{2,1,0:T(8,128)(2,1)}), bf16[32,8,640]{2,1,0:T(8,128)(2,1)S(1)}, u32[]{:S(2)}, u32[]{:S(2)}) async-start(bf16[32,8,640]{2,1,0:T(8,128)(2,1)} %bitcast.12), calls=%async_computation.2 | async-start | bytes 655360 | tf_op jit(solution)/shard_map/all_to_all | solution.py:454
  55.1 4.1 %collective-permute-start.1 = (bf16[256,349]{1,0:T(8,128)(2,1)S(1)}, bf16[256,349]{1,0:T(8,128)(2,1)S(1)}, u32[]{:S(2)}, u32[]{:S(2)}) collective-permute-start(bf16[256,349]{1,0:T(8,128)(2,1)S(1)} %copy-done.1), channel_id=1, source_target_pairs={{0,1},{1,0},{2,3},{3,2},{4,5},{5,4},{6,7},{7,6},{8,9},{9,8},{10,11... | collective-permute-start | bytes 536072 | tf_op jit(solution)/shard_map/ppermute | solution.py:389
  68.7 1.7 %collective-permute-start.3 = (bf16[256,512]{1,0:T(8,128)(2,1)S(1)}, bf16[256,512]{1,0:T(8,128)(2,1)S(1)}, u32[]{:S(2)}, u32[]{:S(2)}) collective-permute-start(bf16[256,512]{1,0:T(8,128)(2,1)S(1)} %get-tuple-element.94.grad_ref), channel_id=1, source_target_pairs={{0,1},{1,0},{2,3},{3,2},{4,5},{5,4},{6,7},{7,6},{8,9},{9,8},{10,11... | collective-permute-start | bytes 786440 | tf_op jit(solution)/shard_map/ppermute | solution.py:389
  70.4 3.5 %copy-start.3 = (bf16[8,48,349]{2,1,0:T(8,128)(2,1)S(1)}, bf16[8,48,349]{2,1,0:T(8,128)(2,1)}, u32[]{:S(2)}) copy-start(bf16[8,48,349]{2,1,0:T(8,128)(2,1)} %get-tuple-element.124) | copy-start | bytes 804100
  70.4 5.2 %copy-start.2 = (bf16[8,48,349]{2,1,0:T(8,128)(2,1)S(1)}, bf16[8,48,349]{2,1,0:T(8,128)(2,1)}, u32[]{:S(2)}) copy-start(bf16[8,48,349]{2,1,0:T(8,128)(2,1)} %get-tuple-element.130) | copy-start | bytes 804100
  70.4 13.0 %copy-start = (bf16[8,48,349]{2,1,0:T(8,128)(2,1)S(1)}, bf16[8,48,349]{2,1,0:T(8,128)(2,1)}, u32[]{:S(2)}) copy-start(bf16[8,48,349]{2,1,0:T(8,128)(2,1)} %get-tuple-element.85.after_ref) | copy-start | bytes 804100
  71.8 11.6 %collective-permute-start.8 = (bf16[8,48,512]{2,1,0:T(8,128)(2,1)S(1)}, bf16[8,48,512]{2,1,0:T(8,128)(2,1)S(1)}, u32[]{:S(2)}, u32[]{:S(2)}) collective-permute-start(bf16[8,48,512]{2,1,0:T(8,128)(2,1)S(1)} %get-tuple-element.103), channel_id=1, source_target_pairs={{0,4},{1,5},{2,6},{3,7},{4,0},{5,1},{6,2},{7,3},{8,12},{9,13},{10,... | collective-permute-start | bytes 1179656 | tf_op jit(solution)/shard_map/ppermute | solution.py:384
  72.6 12.0 %collective-permute-start.11 = (bf16[8,48,512]{2,1,0:T(8,128)(2,1)S(1)}, bf16[8,48,512]{2,1,0:T(8,128)(2,1)S(1)}, u32[]{:S(2)}, u32[]{:S(2)}) collective-permute-start(bf16[8,48,512]{2,1,0:T(8,128)(2,1)S(1)} %get-tuple-element.109), channel_id=1, source_target_pairs={{0,8},{1,9},{2,10},{3,11},{4,12},{5,13},{6,14},{7,15},{8,0},{9,1},... | collective-permute-start | bytes 1179656 | tf_op jit(solution)/shard_map/ppermute | solution.py:384
  73.3 12.1 %collective-permute-start.4 = (bf16[8,48,512]{2,1,0:T(8,128)(2,1)S(1)}, bf16[8,48,512]{2,1,0:T(8,128)(2,1)S(1)}, u32[]{:S(2)}, u32[]{:S(2)}) collective-permute-start(bf16[8,48,512]{2,1,0:T(8,128)(2,1)S(1)} %get-tuple-element.95), channel_id=1, source_target_pairs={{0,2},{1,3},{2,0},{3,1},{4,6},{5,7},{6,4},{7,5},{8,10},{9,11},{10,... | collective-permute-start | bytes 1179656 | tf_op jit(solution)/shard_map/ppermute | solution.py:384
  73.9 17.1 %collective-permute-start.19 = (bf16[8,48,349]{2,1,0:T(8,128)(2,1)S(1)}, bf16[8,48,349]{2,1,0:T(8,128)(2,1)S(1)}, u32[]{:S(2)}, u32[]{:S(2)}) collective-permute-start(bf16[8,48,349]{2,1,0:T(8,128)(2,1)S(1)} %copy-done.3), channel_id=1, source_target_pairs={{0,8},{1,9},{2,10},{3,11},{4,12},{5,13},{6,14},{7,15},{8,0},{9,1},... | collective-permute-start | bytes 804104 | tf_op jit(solution)/shard_map/ppermute | solution.py:384
  75.6 21.7 %collective-permute-start.22 = (bf16[8,48,349]{2,1,0:T(8,128)(2,1)S(1)}, bf16[8,48,349]{2,1,0:T(8,128)(2,1)S(1)}, u32[]{:S(2)}, u32[]{:S(2)}) collective-permute-start(bf16[8,48,349]{2,1,0:T(8,128)(2,1)S(1)} %copy-done.2), channel_id=1, source_target_pairs={{0,8},{1,9},{2,10},{3,11},{4,12},{5,13},{6,14},{7,15},{8,0},{9,1},... | collective-permute-start | bytes 804104 | tf_op jit(solution)/shard_map/ppermute | solution.py:384
  83.4 14.8 %collective-permute-start.15 = (bf16[8,48,349]{2,1,0:T(8,128)(2,1)S(1)}, bf16[8,48,349]{2,1,0:T(8,128)(2,1)S(1)}, u32[]{:S(2)}, u32[]{:S(2)}) collective-permute-start(bf16[8,48,349]{2,1,0:T(8,128)(2,1)S(1)} %copy-done), channel_id=1, source_target_pairs={{0,2},{1,3},{2,0},{3,1},{4,6},{5,7},{6,4},{7,5},{8,10},{9,11},{10,... | collective-permute-start | bytes 804104 | tf_op jit(solution)/shard_map/ppermute | solution.py:384
  84.6 16.1 %collective-permute-start.9 = (bf16[4,48,512]{2,1,0:T(8,128)(2,1)S(1)}, bf16[4,48,512]{2,1,0:T(8,128)(2,1)S(1)}, u32[]{:S(2)}, u32[]{:S(2)}) collective-permute-start(bf16[4,48,512]{2,1,0:T(8,128)(2,1)S(1)} %get-tuple-element.105), channel_id=1, source_target_pairs={{0,8},{1,9},{2,10},{3,11},{4,12},{5,13},{6,14},{7,15},{8,0},{9,1},... | collective-permute-start | bytes 589832 | tf_op jit(solution)/shard_map/ppermute | solution.py:384
  85.4 16.7 %collective-permute-start.12 = (bf16[4,48,512]{2,1,0:T(8,128)(2,1)S(1)}, bf16[4,48,512]{2,1,0:T(8,128)(2,1)S(1)}, u32[]{:S(2)}, u32[]{:S(2)}) collective-permute-start(bf16[4,48,512]{2,1,0:T(8,128)(2,1)S(1)} %get-tuple-element.111), channel_id=1, source_target_pairs={{0,2},{1,3},{2,0},{3,1},{4,6},{5,7},{6,4},{7,5},{8,10},{9,11},{10,... | collective-permute-start | bytes 589832 | tf_op jit(solution)/shard_map/ppermute | solution.py:384
  91.0 11.4 %collective-permute-start.5 = (bf16[4,48,512]{2,1,0:T(8,128)(2,1)S(1)}, bf16[4,48,512]{2,1,0:T(8,128)(2,1)S(1)}, u32[]{:S(2)}, u32[]{:S(2)}) collective-permute-start(bf16[4,48,512]{2,1,0:T(8,128)(2,1)S(1)} %get-tuple-element.97), channel_id=1, source_target_pairs={{0,4},{1,5},{2,6},{3,7},{4,0},{5,1},{6,2},{7,3},{8,12},{9,13},{10,... | collective-permute-start | bytes 589832 | tf_op jit(solution)/shard_map/ppermute | solution.py:384
  97.3 6.7 %collective-permute-start.20 = (bf16[4,48,349]{2,1,0:T(8,128)(2,1)S(1)}, bf16[4,48,349]{2,1,0:T(8,128)(2,1)S(1)}, u32[]{:S(2)}, u32[]{:S(2)}) collective-permute-start(bf16[4,48,349]{2,1,0:T(8,128)(2,1)S(1)} %get-tuple-element.126), channel_id=1, source_target_pairs={{0,2},{1,3},{2,0},{3,1},{4,6},{5,7},{6,4},{7,5},{8,10},{9,11},{10,... | collective-permute-start | bytes 402056 | tf_op jit(solution)/shard_map/ppermute | solution.py:384
  98.3 7.5 %collective-permute-start.23 = (bf16[4,48,349]{2,1,0:T(8,128)(2,1)S(1)}, bf16[4,48,349]{2,1,0:T(8,128)(2,1)S(1)}, u32[]{:S(2)}, u32[]{:S(2)}) collective-permute-start(bf16[4,48,349]{2,1,0:T(8,128)(2,1)S(1)} %get-tuple-element.132), channel_id=1, source_target_pairs={{0,2},{1,3},{2,0},{3,1},{4,6},{5,7},{6,4},{7,5},{8,10},{9,11},{10,... | collective-permute-start | bytes 402056 | tf_op jit(solution)/shard_map/ppermute | solution.py:384
  100.7 6.7 %collective-permute-start.16 = (bf16[4,48,349]{2,1,0:T(8,128)(2,1)S(1)}, bf16[4,48,349]{2,1,0:T(8,128)(2,1)S(1)}, u32[]{:S(2)}, u32[]{:S(2)}) collective-permute-start(bf16[4,48,349]{2,1,0:T(8,128)(2,1)S(1)} %get-tuple-element.118), channel_id=1, source_target_pairs={{0,4},{1,5},{2,6},{3,7},{4,0},{5,1},{6,2},{7,3},{8,12},{9,13},{10,... | collective-permute-start | bytes 402056 | tf_op jit(solution)/shard_map/ppermute | solution.py:384
  102.0 6.7 %collective-permute-start.10 = (bf16[2,48,512]{2,1,0:T(8,128)(2,1)S(1)}, bf16[2,48,512]{2,1,0:T(8,128)(2,1)S(1)}, u32[]{:S(2)}, u32[]{:S(2)}) collective-permute-start(bf16[2,48,512]{2,1,0:T(8,128)(2,1)S(1)} %get-tuple-element.107), channel_id=1, source_target_pairs={{0,2},{1,3},{2,0},{3,1},{4,6},{5,7},{6,4},{7,5},{8,10},{9,11},{10,... | collective-permute-start | bytes 294920 | tf_op jit(solution)/shard_map/ppermute | solution.py:384
  102.4 7.1 %collective-permute-start.13 = (bf16[2,48,512]{2,1,0:T(8,128)(2,1)S(1)}, bf16[2,48,512]{2,1,0:T(8,128)(2,1)S(1)}, u32[]{:S(2)}, u32[]{:S(2)}) collective-permute-start(bf16[2,48,512]{2,1,0:T(8,128)(2,1)S(1)} %get-tuple-element.113), channel_id=1, source_target_pairs={{0,4},{1,5},{2,6},{3,7},{4,0},{5,1},{6,2},{7,3},{8,12},{9,13},{10,... | collective-permute-start | bytes 294920 | tf_op jit(solution)/shard_map/ppermute | solution.py:384
  103.9 9.2 %collective-permute-start.6 = (bf16[2,48,512]{2,1,0:T(8,128)(2,1)S(1)}, bf16[2,48,512]{2,1,0:T(8,128)(2,1)S(1)}, u32[]{:S(2)}, u32[]{:S(2)}) collective-permute-start(bf16[2,48,512]{2,1,0:T(8,128)(2,1)S(1)} %get-tuple-element.99), channel_id=1, source_target_pairs={{0,16},{1,17},{2,18},{3,19},{4,20},{5,21},{6,22},{7,23},{8,24},{9,... | collective-permute-start | bytes 294920 | tf_op jit(solution)/shard_map/ppermute | solution.py:384
  105.8 6.1 %collective-permute-start.21 = (bf16[2,48,349]{2,1,0:T(8,128)(2,1)S(1)}, bf16[2,48,349]{2,1,0:T(8,128)(2,1)S(1)}, u32[]{:S(2)}, u32[]{:S(2)}) collective-permute-start(bf16[2,48,349]{2,1,0:T(8,128)(2,1)S(1)} %get-tuple-element.128), channel_id=1, source_target_pairs={{0,4},{1,5},{2,6},{3,7},{4,0},{5,1},{6,2},{7,3},{8,12},{9,13},{10,... | collective-permute-start | bytes 201032 | tf_op jit(solution)/shard_map/ppermute | solution.py:384
  107.4 4.4 %collective-permute-start.24 = (bf16[2,48,349]{2,1,0:T(8,128)(2,1)S(1)}, bf16[2,48,349]{2,1,0:T(8,128)(2,1)S(1)}, u32[]{:S(2)}, u32[]{:S(2)}) collective-permute-start(bf16[2,48,349]{2,1,0:T(8,128)(2,1)S(1)} %get-tuple-element.134), channel_id=1, source_target_pairs={{0,4},{1,5},{2,6},{3,7},{4,0},{5,1},{6,2},{7,3},{8,12},{9,13},{10,... | collective-permute-start | bytes 201032 | tf_op jit(solution)/shard_map/ppermute | solution.py:384
  108.8 9.5 %collective-permute-start.17 = (bf16[2,48,349]{2,1,0:T(8,128)(2,1)S(1)}, bf16[2,48,349]{2,1,0:T(8,128)(2,1)S(1)}, u32[]{:S(2)}, u32[]{:S(2)}) collective-permute-start(bf16[2,48,349]{2,1,0:T(8,128)(2,1)S(1)} %get-tuple-element.120), channel_id=1, source_target_pairs={{0,16},{1,17},{2,18},{3,19},{4,20},{5,21},{6,22},{7,23},{8,24},{9,... | collective-permute-start | bytes 201032 | tf_op jit(solution)/shard_map/ppermute | solution.py:384
  109.5 13.5 %collective-permute-start.14 = (bf16[96,512]{1,0:T(8,128)(2,1)S(1)}, bf16[96,512]{1,0:T(8,128)(2,1)S(1)}, u32[]{:S(2)}, u32[]{:S(2)}) collective-permute-start(bf16[96,512]{1,0:T(8,128)(2,1)S(1)} %get-tuple-element.115), channel_id=1, source_target_pairs={{0,16},{1,17},{2,18},{3,19},{4,20},{5,21},{6,22},{7,23},{8,24},{9,... | collective-permute-start | bytes 294920 | tf_op jit(solution)/shard_map/ppermute | solution.py:384
  111.9 10.4 %collective-permute-start.25 = (bf16[96,349]{1,0:T(8,128)(2,1)S(1)}, bf16[96,349]{1,0:T(8,128)(2,1)S(1)}, u32[]{:S(2)}, u32[]{:S(2)}) collective-permute-start(bf16[96,349]{1,0:T(8,128)(2,1)S(1)} %get-tuple-element.136), channel_id=1, source_target_pairs={{0,16},{1,17},{2,18},{3,19},{4,20},{5,21},{6,22},{7,23},{8,24},{9,... | collective-permute-start | bytes 201032 | tf_op jit(solution)/shard_map/ppermute | solution.py:384
  113.1 9.9 %collective-permute-start.7 = (bf16[48,512]{1,0:T(8,128)(2,1)S(1)}, bf16[48,512]{1,0:T(8,128)(2,1)S(1)}, u32[]{:S(2)}, u32[]{:S(2)}) collective-permute-start(bf16[48,512]{1,0:T(8,128)(2,1)S(1)} %get-tuple-element.101), channel_id=1, source_target_pairs={{0,8},{1,9},{2,10},{3,11},{4,12},{5,13},{6,14},{7,15},{8,0},{9,1},... | collective-permute-start | bytes 147464 | tf_op jit(solution)/shard_map/ppermute | solution.py:384
  118.3 4.0 %collective-permute-start.18 = (bf16[48,349]{1,0:T(8,128)(2,1)S(1)}, bf16[48,349]{1,0:T(8,128)(2,1)S(1)}, u32[]{:S(2)}, u32[]{:S(2)}) collective-permute-start(bf16[48,349]{1,0:T(8,128)(2,1)S(1)} %get-tuple-element.122), channel_id=1, source_target_pairs={{0,8},{1,9},{2,10},{3,11},{4,12},{5,13},{6,14},{7,15},{8,0},{9,1},... | collective-permute-start | bytes 100520 | tf_op jit(solution)/shard_map/ppermute | solution.py:384
